TPU v7x, 32 devices: a whole 2x2x4 slice. The times are simulated.
32 devices in a mesh: gx: 4 (over x, core), gy: 4 (over z), gz: 2 (over y).
Axes of the slice: x: 2, y: 2, z: 4, core: 2. Of those that a mesh axis runs over, the one named last changes fastest.
Arguments:
- layer_input: bfloat16 [1024, 4096], P('gz', ('gx', 'gy')), may hold values from -6 to 6
- modality: int32 [1024], P('gz'), may hold values 0 or 1
- image_spans: int32 [2, 8], replicated, may hold values from 0 to 1024, as said below
- norm_gain: float32 [2, 4096], P(None, ('gx', 'gy')), may hold values from 0.1 to 1.9
- w_qkv: bfloat16 [3, 4096, 2048], P(None, 'gz', ('gx', 'gy')), as said below
- w_out: bfloat16 [2048, 4096], P(('gx', 'gy'), 'gz'), may hold values from -0.125 to 0.125
- grad_out: bfloat16 [1024, 4096], P('gz', ('gx', 'gy')), may hold values from -6 to 6
Outputs:
- attn_out: bfloat16 [1024, 4096], P('gz', ('gx', 'gy'))
- grad_in: bfloat16 [1024, 4096], P('gz', ('gx', 'gy'))
- grad_qkv: float32 [3, 4096, 2048], P(None, 'gz', ('gx', 'gy'))
- grad_wout: float32 [2048, 4096], P(('gx', 'gy'), 'gz')
- grad_gain: float32 [2, 4096], P(None, ('gx', 'gy'))
Inputs may be any that keep to these rules, and one draw needn't show every extreme that they name: `image_spans`: row 0 holds the first position of each of 8 image spans, in increasing order, and row 1 one past its last; spans are disjoint and none is empty. `w_qkv`: entries are at most 20 * 4096 ** -0.5 in magnitude.
All inputs are finite; a program needn't handle non-finite values. No bound on the sum of `modality` on one device may be relied on, other than what follows from the above.
Results may differ from a plain program's by a relative error of at most 0.035.
The roundings to bfloat16 on the way count: a program that leaves them out, or rounds other values in their place, can miss the bound.
Values may be sent and summed in bfloat16 or wider, within the bound.
A program may use at most 128 MiB of HBM per device.

v0:
```python
import math

import jax
import jax.numpy as jnp
from jax import lax
from jax.sharding import PartitionSpec as P

epsilon = 1e-05
masked_low = -1e30


def span_index(positions, image_spans):
    inside = (positions[:, None] >= image_spans[0][None, :]) & (
        positions[:, None] < image_spans[1][None, :]
    )
    labels = jnp.arange(1, image_spans.shape[1] + 1, dtype=jnp.int32)
    return jnp.sum(jnp.where(inside, labels[None, :], 0), axis=1) - 1


def visible(query_pos, query_span, key_pos, key_span):
    causal = key_pos[None, :] <= query_pos[:, None]
    same_image = (query_span[:, None] == key_span[None, :]) & (query_span[:, None] >= 0)
    return causal | same_image


def per_device(layer_input, modality, image_spans, norm_gain, w_qkv, w_out, grad_out):
    tok_rows, local_width = layer_input.shape
    full_width = local_width * lax.axis_size(("gx", "gy"))
    head_dim = w_qkv.shape[2]
    inputs_f = layer_input.astype(jnp.float32)
    squares = lax.psum(jnp.sum(inputs_f * inputs_f, axis=1), ("gx", "gy"))
    inv_rms = lax.rsqrt(squares / full_width + epsilon)
    row_gain = jnp.where(modality[:, None] == 1, norm_gain[1][None, :], norm_gain[0][None, :])
    scaled = inputs_f * inv_rms[:, None]
    normed = (scaled * row_gain).astype(jnp.bfloat16)
    w_full = lax.all_gather(w_qkv, "gz", axis=1, tiled=True)
    wo_full = lax.all_gather(w_out, "gz", axis=1, tiled=True)
    rows_block = w_full
    projected = jnp.einsum(
        "tc,mch->mth",
        lax.all_gather(normed, ("gx", "gy"), axis=1, tiled=True),
        rows_block,
        preferred_element_type=jnp.float32,
    )
    projected = projected.astype(jnp.bfloat16)
    queries = projected[0]
    keys_values = lax.all_gather(
        jnp.concatenate([projected[1], projected[2]], axis=1), "gz", axis=0, tiled=True
    )
    key_total = keys_values.shape[0]
    query_pos = lax.axis_index("gz") * tok_rows + jnp.arange(tok_rows, dtype=jnp.int32)
    query_span = span_index(query_pos, image_spans)
    key_block = 512
    block_count = key_total // key_block
    score_scale = 1.0 / math.sqrt(head_dim)
    block_ids = jnp.arange(block_count, dtype=jnp.int32)

    def block_scores(block_idx):
        first_key = block_idx * key_block
        kv_block = lax.dynamic_slice_in_dim(keys_values, first_key, key_block, 0)
        key_pos = first_key + jnp.arange(key_block, dtype=jnp.int32)
        allowed = visible(query_pos, query_span, key_pos, span_index(key_pos, image_spans))
        scores = (
            lax.dot_general(
                queries,
                kv_block[:, :head_dim],
                (((1,), (1,)), ((), ())),
                preferred_element_type=jnp.float32,
            )
            * score_scale
        )
        return (kv_block, allowed, scores)

    def gather_stats(state, block_idx):
        maxima, summed = state
        kv_block, allowed, scores = block_scores(block_idx)
        new_maxima = jnp.maximum(maxima, jnp.max(jnp.where(allowed, scores, masked_low), axis=1))
        fresh = jnp.sum(jnp.where(allowed, jnp.exp(scores - new_maxima[:, None]), 0.0), axis=1)
        return ((new_maxima, summed * jnp.exp(maxima - new_maxima) + fresh), None)

    start_state = (
        jnp.full((tok_rows,), masked_low, jnp.float32),
        jnp.zeros((tok_rows,), jnp.float32),
    )
    (maxima, summed), unused = lax.scan(gather_stats, start_state, block_ids)
    lse = maxima + jnp.log(summed)

    def block_probs(block_idx):
        kv_block, allowed, scores = block_scores(block_idx)
        return (kv_block, jnp.where(allowed, jnp.exp(scores - lse[:, None]), 0.0))

    def attend(accum, block_idx):
        kv_block, attn_p = block_probs(block_idx)
        return (
            accum
            + jnp.dot(
                attn_p.astype(jnp.bfloat16),
                kv_block[:, head_dim:],
                preferred_element_type=jnp.float32,
            ),
            None,
        )

    attended_f, unused = lax.scan(attend, jnp.zeros((tok_rows, head_dim), jnp.float32), block_ids)
    attended = attended_f.astype(jnp.bfloat16)
    all_heads = lax.all_gather(attended, ("gx", "gy"), axis=1, tiled=True)
    out_rows = lax.all_to_all(wo_full, ("gx", "gy"), split_axis=1, concat_axis=0, tiled=True)
    head_total = out_rows.shape[0] // head_dim
    per_head = jnp.einsum(
        "thd,hdc->htc",
        all_heads.reshape(tok_rows, head_total, head_dim),
        out_rows.reshape(head_total, head_dim, local_width),
        preferred_element_type=jnp.float32,
    )
    per_head = lax.optimization_barrier(per_head.astype(jnp.bfloat16)).astype(jnp.float32)
    attn_out = jnp.sum(per_head, axis=0).astype(jnp.bfloat16)
    segment = lax.all_gather(grad_out, ("gx", "gy"), axis=1, tiled=True)
    d_accum = lax.dot_general(
        segment, wo_full, (((1,), (1,)), ((), ())), preferred_element_type=jnp.float32
    )
    partial_value = lax.dot_general(
        attended, segment, (((0,), (0,)), ((), ())), preferred_element_type=jnp.float32
    )
    d_attended = d_accum.astype(jnp.bfloat16)
    row_dots = jnp.sum(d_attended.astype(jnp.float32) * attended.astype(jnp.float32), axis=1)

    def backward_block(d_query, block_idx):
        kv_block, attn_p = block_probs(block_idx)
        d_probs = lax.dot_general(
            d_attended,
            kv_block[:, head_dim:],
            (((1,), (1,)), ((), ())),
            preferred_element_type=jnp.float32,
        )
        d_scores = (attn_p * (d_probs - row_dots[:, None]) * score_scale).astype(jnp.bfloat16)
        d_query = d_query + jnp.dot(
            d_scores, kv_block[:, :head_dim], preferred_element_type=jnp.float32
        )
        d_keys = lax.dot_general(
            d_scores, queries, (((0,), (0,)), ((), ())), preferred_element_type=jnp.float32
        )
        d_values = lax.dot_general(
            attn_p.astype(jnp.bfloat16),
            d_attended,
            (((0,), (0,)), ((), ())),
            preferred_element_type=jnp.float32,
        )
        return (d_query, jnp.concatenate([d_keys, d_values], axis=1))

    d_query_f, kv_parts = lax.scan(
        backward_block, jnp.zeros((tok_rows, head_dim), jnp.float32), block_ids
    )
    kv_grad = lax.psum_scatter(
        kv_parts.reshape(key_total, 2 * head_dim).astype(jnp.bfloat16),
        "gz",
        scatter_dimension=0,
        tiled=True,
    ).astype(jnp.float32)
    grads = jnp.stack(
        [
            d_query_f.astype(jnp.bfloat16),
            kv_grad[:, :head_dim].astype(jnp.bfloat16),
            kv_grad[:, head_dim:].astype(jnp.bfloat16),
        ]
    )
    w_grad = jnp.einsum(
        "tc,mth->mch",
        lax.all_gather(normed, ("gx", "gy"), axis=1, tiled=True),
        grads,
        preferred_element_type=jnp.float32,
    )
    grad_qkv, grad_wout = (
        lax.psum_scatter(w_grad.astype(jnp.bfloat16), "gz", scatter_dimension=1, tiled=True).astype(
            jnp.float32
        ),
        lax.psum_scatter(
            partial_value.astype(jnp.bfloat16), "gz", scatter_dimension=1, tiled=True
        ).astype(jnp.float32),
    )
    rows_block = w_full
    grad_normed = (
        lax.psum_scatter(
            jnp.einsum("mch,mth->ct", rows_block, grads, preferred_element_type=jnp.float32).astype(
                jnp.bfloat16
            ),
            ("gx", "gy"),
            scatter_dimension=0,
            tiled=True,
        )
        .astype(jnp.float32)
        .T
    )
    upstream = grad_normed * row_gain
    norm_dots = lax.psum(jnp.sum(upstream * scaled, axis=1), ("gx", "gy"))
    grad_in = (inv_rms[:, None] * (upstream - scaled * (norm_dots / full_width)[:, None])).astype(
        jnp.bfloat16
    )
    onehot = (modality[:, None] == jnp.arange(2, dtype=jnp.int32)[None, :]).astype(jnp.float32)
    local_gain = jnp.dot(onehot.T, grad_normed * scaled, precision=lax.Precision.HIGHEST)
    grad_gain = lax.psum(local_gain, "gz")
    return (attn_out, grad_in, grad_qkv, grad_wout, grad_gain)


def solution(mesh):
    in_specs = (
        P("gz", ("gx", "gy")),
        P("gz"),
        P(),
        P(None, ("gx", "gy")),
        P(None, "gz", ("gx", "gy")),
        P(("gx", "gy"), "gz"),
        P("gz", ("gx", "gy")),
    )
    out_specs = (
        P("gz", ("gx", "gy")),
        P("gz", ("gx", "gy")),
        P(None, "gz", ("gx", "gy")),
        P(("gx", "gy"), "gz"),
        P(None, ("gx", "gy")),
    )
    return jax.shard_map(
        per_device, mesh=mesh, in_specs=in_specs, out_specs=out_specs, check_vma=False
    )
```

profile of v0, /device:TPU:0, one launch (start us, length us, event | category | flops | bytes accessed | tf_op | source)
XLA Modules:
  0.0 420.7 jit_solution(4267195177550142330)
XLA Ops:
  10.2 35.2 %psum.21 = f32[512]{0:T(512)S(1)} all-reduce(f32[512]{0:T(512)S(1)} %fusion.65), channel_id=1, replica_groups=mesh['gx'=4,'gy'=4,'gz'=2] {'gx','gy'}, use_global_device_ids=true, to_apply=%region_1.0 | all-reduce | flops 512 | bytes 4096 | tf_op jit(solution)/shard_map/psum | solution.py:31
  48.3 9.5 %all-gather.8.cloned.1.call-done = bf16[3,4096,128]{1,2,0:T(8,128)(2,1)} async-done(((bf16[3,2048,128]{1,2,0:T(8,128)(2,1)}), bf16[3,4096,128]{1,2,0:T(8,128)(2,1)}) %all-gather.8.cloned.1.call-update) | async-done | bytes 3145744 | tf_op jit(solution)/shard_map/all_gather | solution.py:36
  57.8 55.2 %all-gather.6.cloned.1.call-done = bf16[512,4096]{1,0:T(8,128)(2,1)} async-done(((bf16[512,256]{1,0:T(8,128)(2,1)}), bf16[512,4096]{1,0:T(8,128)(2,1)}) %all-gather.6.cloned.1.call-update) | async-done | bytes 4194320 | tf_op jit(solution)/shard_map/all_gather | solution.py:41
  113.0 5.0 %fusion.75 = f32[512,384]{0,1:S(1)} fusion(bf16[512,4096]{1,0:T(8,128)(2,1)} %all-gather.6.cloned.1.call-done, bf16[4096,384]{0,1:T(8,128)(2,1)} %bitcast.156), kind=kOutput, calls=%fused_computation.134 | convolution fusion | flops 1610612736 | bytes 8126464
  118.1 13.9 %all_gather.21 = bf16[1024,256]{0,1:T(8,128)(2,1)S(1)} all-gather(bf16[512,256]{0,1:T(8,128)(2,1)S(1)} %pad_maximum_fusion.1), channel_id=1, replica_groups=mesh['gx'=4,'gy'=4,'gz'=2] {'gz'}, dimensions={0}, use_global_device_ids=true | all-gather | bytes 786432 | tf_op jit(solution)/shard_map/all_gather | solution.py:47
  132.4 4.8 %while.43 = (s32[]{:T(128)}, f32[512]{0:T(512)S(1)}, f32[512]{0:T(512)S(1)}, s32[2]{0:T(128)S(1)}, s32[512]{0:T(512)S(1)}, /*index=5*/s32[2,8]{1,0:T(2,128)S(1)}...) while((s32[]{:T(128)}, f32[512]{0:T(512)S(1)}, ...), condition=%wide.region_7.8_spmd.clone, body=%wide.region_3.7_spmd.clone.sunk | while | flops 70803472 | bytes 2418638 | solution.py:85
  137.7 5.9 %while.44 = (s32[]{:T(128)}, f32[512,128]{1,0:T(8,128)S(1)}, s32[2]{0:T(128)S(1)}, s32[512]{0:T(512)S(1)}, s32[2,8]{1,0:T(2,128)S(1)}, /*index=5*/bf16[1024,256]...) while((s32[]{:T(128)}, f32[512,128]{1,0:T(8,128)S(1)}, ...), condition=%wide.region_10.11_spmd.clone, body=%wide.region_8.10_spmd.clone.sunk | while | flops 136467984 | bytes 945628 | solution.py:104
  143.8 47.6 %all-gather.14.cloned.1.call-done = bf16[512,4096]{1,0:T(8,128)(2,1)} async-done(((bf16[512,256]{1,0:T(8,128)(2,1)}), bf16[512,4096]{1,0:T(8,128)(2,1)}) %all-gather.14.cloned.1.call-update) | async-done | bytes 4194320 | tf_op jit(solution)/shard_map/all_gather | solution.py:117
  191.3 4.0 multiply_reduce_fusion
  196.0 9.3 %while.45 = (s32[]{:T(128)}, f32[512,128]{1,0:T(8,128)S(1)}, bf16[2,512,256]{1,2,0:T(8,128)(2,1)S(1)}, s32[2]{0:T(128)}, s32[512]{0:T(512)S(1)}, /*index=5*/s32[...) while((s32[]{:T(128)}, f32[512,128]{1,0:T(8,128)S(1)}, ...), condition=%wide.region_15.16_spmd.clone, body=%wide.region_13.15_spmd.clone.sunk | while | flops 339367424 | bytes 6974985 | solution.py:150
  206.4 3.9 convolution_convert_fusion.1
  211.1 8.2 %reduce-scatter.5.cloned.1.call-done = bf16[512,256]{1,0:T(8,128)(2,1)} async-done(((bf16[1024,256]{1,0:T(8,128)(2,1)}), bf16[512,256]{1,0:T(8,128)(2,1)}) %reduce-scatter.5.cloned.1.call-update) | async-done | bytes 262160 | tf_op jit(solution)/shard_map/reduce_scatter | solution.py:153
  220.2 5.8 %fusion.52 = bf16[4096,512]{0,1:T(8,128)(2,1)} fusion(bf16[3,4096,128]{1,2,0:T(8,128)(2,1)} %all-gather.8.cloned.1.call-done, bf16[1,512,128]{2,1,0:T(8,128)(2,1)S(1)} %get-tuple-element.678, bf16[1,512,128]{2,1,0:T(8,128)(2,1)S(1)} %get-tuple-element.677, bf16[1,512,128]{2,1,0:T(8,128)(2,1)S(1)} %convert_bitcast_fusion.1), kind=kOutput, calls=%fused_computation.84 | convolution fusion | flops 1613103104 | bytes 7733248 | tf_op jit(solution)/shard_map/mch,mth->ct/dot_general | solution.py:183
  226.3 6.1 %fusion.53 = bf16[3,4096,128]{1,2,0:T(8,128)(2,1)} fusion(bf16[512,4096]{1,0:T(8,128)(2,1)} %all-gather.6.cloned.1.call-done, bf16[1,512,128]{2,1,0:T(8,128)(2,1)S(1)} %get-tuple-element.678, bf16[1,512,128]{2,1,0:T(8,128)(2,1)S(1)} %get-tuple-element.677, bf16[1,512,128]{2,1,0:T(8,128)(2,1)S(1)} %convert_bitcast_fusion.1), kind=kOutput, calls=%fused_computation.85 | convolution fusion | flops 1612578816 | bytes 7733248 | tf_op jit(solution)/shard_map/tc,mth->mch/dot_general | solution.py:166
  233.8 5.5 %all-to-all-start = ((bf16[128,16,256]{2,0,1:T(8,128)(2,1)}), bf16[128,16,256]{2,0,1:T(8,128)(2,1)S(1)}, u32[]{:S(2)}, u32[]{:S(2)}) async-start(bf16[128,16,256]{2,0,1:T(8,128)(2,1)} %copy.51), calls=%async_computation | async-start | bytes 2097152 | tf_op jit(solution)/shard_map/all_to_all | solution.py:107
  239.3 3.1 reduce-scatter.11.cloned.1.call-done
  244.5 25.8 %all-to-all-done = bf16[128,16,256]{2,0,1:T(8,128)(2,1)S(1)} async-done(((bf16[128,16,256]{2,0,1:T(8,128)(2,1)}), bf16[128,16,256]{2,0,1:T(8,128)(2,1)S(1)}, u32[]{:S(2)}, u32[]{:S(2)}) %all-to-all-start) | async-done | bytes 1048608 | tf_op jit(solution)/shard_map/all_to_all | solution.py:107
  270.3 19.1 %all-gather.10.cloned.1.call-done = bf16[512,2048]{0,1:T(8,128)(2,1)} async-done(((bf16[512,128]{0,1:T(8,128)(2,1)}), bf16[512,2048]{0,1:T(8,128)(2,1)}) %all-gather.10.cloned.1.call-update) | async-done | bytes 2097168 | tf_op jit(solution)/shard_map/all_gather | solution.py:106
  289.4 4.8 %convolution_convert_fusion.2 = bf16[16,512,256]{2,1,0:T(8,128)(2,1)} fusion(bf16[512,16,128]{0,2,1:T(8,128)(2,1)} %bitcast.147, bf16[128,16,256]{2,0,1:T(8,128)(2,1)S(1)} %all-to-all-done), kind=kOutput, calls=%fused_computation.88 | convolution fusion | flops 538968064 | bytes 7340032 | tf_op jit(solution)/shard_map/thd,hdc->htc/dot_general | solution.py:109
  294.2 3.5 reduce_sum.98
  297.8 67.0 %reduce-scatter.7.cloned.1.call-done = bf16[256,512]{0,1:T(8,128)(2,1)} async-done(((bf16[4096,512]{0,1:T(8,128)(2,1)}), bf16[256,512]{0,1:T(8,128)(2,1)}) %reduce-scatter.7.cloned.1.call-update) | async-done | bytes 262160 | tf_op jit(solution)/shard_map/reduce_scatter | solution.py:182
  366.1 30.5 %psum.22 = f32[512]{0:T(512)S(1)} all-reduce(f32[512]{0:T(512)S(1)} %fusion.59), channel_id=1, replica_groups=mesh['gx'=4,'gy'=4,'gz'=2] {'gx','gy'}, use_global_device_ids=true, to_apply=%region_19.20 | all-reduce | flops 512 | bytes 4096 | tf_op jit(solution)/shard_map/psum | solution.py:194
  398.1 5.7 %psum.23 = f32[2,256]{1,0:T(2,128)} all-reduce(f32[2,256]{1,0:T(2,128)S(1)} %fusion.63), channel_id=1, replica_groups=mesh['gx'=4,'gy'=4,'gz'=2] {'gz'}, use_global_device_ids=true, to_apply=%region_22.23 | all-reduce | flops 512 | bytes 4096 | tf_op jit(solution)/shard_map/psum | solution.py:200
  403.8 6.4 %reduce-scatter.9.cloned.1.call-done = bf16[3,2048,128]{1,2,0:T(8,128)(2,1)} async-done(((bf16[3,4096,128]{1,2,0:T(8,128)(2,1)}), bf16[3,2048,128]{1,2,0:T(8,128)(2,1)}) %reduce-scatter.9.cloned.1.call-update) | async-done | bytes 1572880 | tf_op jit(solution)/shard_map/reduce_scatter | solution.py:173
  (153 shorter events, 36.5 us)
Async XLA Ops:
  7.2 2.8 copy-start
  7.2 38.2 %copy-start.12 = (s32[512]{0:T(512)S(1)}, s32[512]{0:T(512)}, u32[]{:S(2)}) copy-start(s32[512]{0:T(512)} %param.14) | copy-start | bytes 6148
  7.2 38.2 %copy-start.14 = (f32[2,256]{1,0:T(2,128)S(1)}, f32[2,256]{1,0:T(2,128)}, u32[]{:S(2)}) copy-start(f32[2,256]{1,0:T(2,128)} %param.16) | copy-start | bytes 6148
  7.2 39.2 %copy-start.4 = (bf16[128,2048]{1,0:T(8,128)(2,1)S(1)}, bf16[128,2048]{1,0:T(8,128)(2,1)}, u32[]{:S(2)}) copy-start(bf16[128,2048]{1,0:T(8,128)(2,1)} %param.18) | copy-start | bytes 1572868
  7.2 41.0 %copy-start.5 = (s32[2,8]{1,0:T(2,128)S(1)}, s32[2,8]{1,0:T(2,128)}, u32[]{:S(2)}) copy-start(s32[2,8]{1,0:T(2,128)} %param.15) | copy-start | bytes 196
  7.2 50.6 %all-gather.8.cloned.1.call-start = ((), (), s32[]{:S(2)}) async-start(), calls=%async_computation.6 | async-start | bytes 4718592 | tf_op jit(solution)/shard_map/all_gather | solution.py:36
  10.0 103.0 %all-gather.6.cloned.1.call-start = ((), (), s32[]{:S(2)}) async-start(), calls=%async_computation.5 | async-start | bytes 4456448 | tf_op jit(solution)/shard_map/all_gather | solution.py:41
  45.4 2.8 copy-start.10
  45.4 72.6 %copy-start.6 = (f32[1,256]{1,0:T(1,128)}, f32[1,256]{1,0:T(1,128)S(1)}, u32[]{:S(2)}) copy-start(f32[1,256]{1,0:T(1,128)S(1)} %get-tuple-element.679) | copy-start | bytes 3076
  46.3 97.4 %all-gather.12.cloned.1.call-start = ((), (), s32[]{:S(2)}) async-start(), calls=%async_computation.8 | async-start | bytes 1572864 | tf_op jit(solution)/shard_map/all_gather | solution.py:37
  47.4 143.9 %all-gather.14.cloned.1.call-start = ((), (), s32[]{:S(2)}) async-start(), calls=%async_computation.9 | async-start | bytes 4456448 | tf_op jit(solution)/shard_map/all_gather | solution.py:117
  48.0 171.2 %reduce-scatter.5.cloned.1.call-start = ((), (), s32[]{:S(2)}) async-start(), calls=%async_computation.10 | async-start | bytes 786432 | tf_op jit(solution)/shard_map/reduce_scatter | solution.py:153
  143.7 62.6 %copy-start.2 = (bf16[512,128]{0,1:T(8,128)(2,1)}, bf16[512,128]{0,1:T(8,128)(2,1)S(1)}, u32[]{:S(2)}) copy-start(bf16[512,128]{0,1:T(8,128)(2,1)S(1)} %copy.49) | copy-start | bytes 393220
  206.3 36.1 %reduce-scatter.11.cloned.1.call-start = ((), (), s32[]{:S(2)}) async-start(), calls=%async_computation.13 | async-start | bytes 1572864 | tf_op jit(solution)/shard_map/reduce_scatter | solution.py:176
  210.3 79.1 %all-gather.10.cloned.1.call-start = ((), (), s32[]{:S(2)}) async-start(), calls=%async_computation.7 | async-start | bytes 2228224 | tf_op jit(solution)/shard_map/all_gather | solution.py:106
  211.0 153.8 %reduce-scatter.7.cloned.1.call-start = ((), (), s32[]{:S(2)}) async-start(), calls=%async_computation.11 | async-start | bytes 4456448 | tf_op jit(solution)/shard_map/reduce_scatter | solution.py:182
  226.1 6.4 %copy-start.1 = (bf16[128,4096]{0,1:T(8,128)(2,1)S(1)}, bf16[128,4096]{0,1:T(8,128)(2,1)}, u32[]{:S(2)}) copy-start(bf16[128,4096]{0,1:T(8,128)(2,1)} %all-gather.12.cloned.1.call-done) | copy-start | bytes 3145732
  226.1 184.1 %reduce-scatter.9.cloned.1.call-start = ((), (), s32[]{:S(2)}) async-start(), calls=%async_computation.12 | async-start | bytes 4718592 | tf_op jit(solution)/shard_map/reduce_scatter | solution.py:173
  233.8 36.5 %all-to-all-start = ((bf16[128,16,256]{2,0,1:T(8,128)(2,1)}), bf16[128,16,256]{2,0,1:T(8,128)(2,1)S(1)}, u32[]{:S(2)}, u32[]{:S(2)}) async-start(bf16[128,16,256]{2,0,1:T(8,128)(2,1)} %copy.51), calls=%async_computation | async-start | bytes 2097152 | tf_op jit(solution)/shard_map/all_to_all | solution.py:107
  289.4 75.4 %copy-start.7 = (f32[1,256]{1,0:T(1,128)S(1)}, f32[1,256]{1,0:T(1,128)}, u32[]{:S(2)}) copy-start(f32[1,256]{1,0:T(1,128)} %copy-done.6) | copy-start | bytes 3076
  289.4 75.4 %copy-start.9 = (f32[1,256]{1,0:T(1,128)S(1)}, f32[1,256]{1,0:T(1,128)}, u32[]{:S(2)}) copy-start(f32[1,256]{1,0:T(1,128)} %copy-done.8) | copy-start | bytes 3076
  289.4 75.4 %copy-start.11 = (pred[512]{0:T(512)(128)(4,1)S(1)}, pred[512]{0:T(512)(128)(4,1)}, u32[]{:S(2)}) copy-start(pred[512]{0:T(512)(128)(4,1)} %copy-done.10) | copy-start | bytes 1540
  294.2 102.4 %copy-start.13 = (s32[512]{0:T(512)S(1)}, s32[512]{0:T(512)}, u32[]{:S(2)}) copy-start(s32[512]{0:T(512)} %param.14) | copy-start | bytes 6148
  364.8 48.5 %copy-start.3 = (bf16[256,512]{0,1:T(8,128)(2,1)S(1)}, bf16[256,512]{0,1:T(8,128)(2,1)}, u32[]{:S(2)}) copy-start(bf16[256,512]{0,1:T(8,128)(2,1)} %reduce-scatter.7.cloned.1.call-done) | copy-start | bytes 786436
  (1 other events, 2.7 us)
Sparse Core Ops, SparseCore 0:
  10.1 47.6 all-gather.7
  60.5 52.4 all-gather.5
  115.1 23.5 all-gather.11
  140.6 50.6 all-gather.13
  206.4 12.7 reduce-scatter.4
  221.9 20.3 reduce-scatter.10
  245.1 44.2 all-gather.9
  293.3 71.4 reduce-scatter.6
  367.6 42.5 reduce-scatter.8
where the time goes:
time: 421 us
  waiting for transfers between devices  243 us (58%)
  blocking collectives  85.3 us (20%)
  matrix products  40.2 us (10%)
  local copies, waits for them, and re-layouts  16.1 us (4%)
  between operations  14.2 us (3%)
  other arithmetic  11.5 us (3%)
  starting transfers between devices  6.02 us (1%)
  loops' own time  4.31 us (1%)
    reduce_scatter x1, waiting for transfers between devices, per_device(): lax.psum_scatter(jnp.einsum('mch,mth->ct', rows_block, grads, preferred_e...  67 us
    all_gather x1, waiting for transfers between devices, per_device(): lax.all_gather(normed, ('gx', 'gy'), axis=1, tiled=True)  55.2 us
    all_gather x1, waiting for transfers between devices, per_device(): segment = lax.all_gather(grad_out, ('gx', 'gy'), axis=1, tiled=True)  47.6 us
    psum x1, blocking collectives, per_device(): squares = lax.psum(jnp.sum(inputs_f * inputs_f, axis=1), ('gx', 'gy'))  35.2 us
    psum x1, blocking collectives, per_device(): norm_dots = lax.psum(jnp.sum(upstream * scaled, axis=1), ('gx', 'gy'))  30.5 us
    all_to_all x1, waiting for transfers between devices, per_device(): lax.all_to_all(wo_full, ('gx', 'gy'), split_axis=1, concat_axis=0, tiled=...  25.8 us
    all_gather x1, waiting for transfers between devices, per_device(): all_heads = lax.all_gather(attended, ('gx', 'gy'), axis=1, tiled=True)  19.1 us
    all_gather x1, blocking collectives, per_device(): lax.all_gather(jnp.concatenate([projected[1], projected[2]], axis=1), 'gz...  13.9 us
  transfers between devices with their start and end apart: 10, of which 9 were waited for; matrix products, arithmetic and copies ran while one was open for 11% of the time, Pallas kernels for 0%

commit v1 on v0

v1 whole, which is shorter than its diff:
```python
import functools
import math

import jax
import jax.numpy as jnp
from jax import lax
from jax.sharding import PartitionSpec as P

epsilon = 1e-05
masked_low = -1e30


def span_index(positions, image_spans):
    inside = (positions[:, None] >= image_spans[0][None, :]) & (
        positions[:, None] < image_spans[1][None, :]
    )
    labels = jnp.arange(1, image_spans.shape[1] + 1, dtype=jnp.int32)
    return jnp.sum(jnp.where(inside, labels[None, :], 0), axis=1) - 1


def visible(query_pos, query_span, key_pos, key_span):
    causal = key_pos[None, :] <= query_pos[:, None]
    same_image = (query_span[:, None] == key_span[None, :]) & (query_span[:, None] >= 0)
    return causal | same_image


def shift_ring(block, step):
    count = lax.axis_size("gz")
    return lax.ppermute(block, "gz", [(src, (src + step) % count) for src in range(count)])


def ring_blocks(block):
    return [block] + [shift_ring(block, -step) for step in range(1, lax.axis_size("gz"))]


def ring_reduce(chunk_of):
    moved = [
        shift_ring(chunk_of(step).astype(jnp.bfloat16), step)
        for step in range(1, lax.axis_size("gz"))
    ]
    total = chunk_of(0)
    for term in moved:
        total = total + term.astype(jnp.float32)
    return total


def gather_features(block):
    return lax.all_gather(block, ("gx", "gy"), axis=1, tiled=True)


def per_device(layer_input, modality, image_spans, norm_gain, w_qkv, w_out, grad_out):
    f32, bf16 = jnp.float32, jnp.bfloat16
    tok_rows, local_width = layer_input.shape
    head_dim = w_qkv.shape[2]
    half = w_qkv.shape[1]
    count = lax.axis_size("gz")
    mine = lax.axis_index("gz")
    score_scale = 1.0 / math.sqrt(head_dim)
    owners = [lax.rem(mine + step, count) for step in range(count)]

    w_blocks = ring_blocks(w_qkv)
    wo_blocks = ring_blocks(w_out)
    x_full = gather_features(layer_input)
    gain_full = gather_features(norm_gain)
    go_full = gather_features(grad_out)
    full_width = x_full.shape[1]

    x_f = x_full.astype(f32)
    inv_rms = lax.rsqrt(jnp.sum(x_f * x_f, axis=1) / full_width + epsilon)
    picked = modality[:, None] == 1
    normed = (
        (x_f * inv_rms[:, None]) * jnp.where(picked, gain_full[1][None, :], gain_full[0][None, :])
    ).astype(bf16)

    def columns_of(matrix, step):
        return lax.dynamic_slice_in_dim(matrix, owners[step] * half, half, 1)

    projected = 0.0
    for step in range(count):
        projected = projected + jnp.einsum(
            "tc,mch->mth", columns_of(normed, step), w_blocks[step], preferred_element_type=f32
        )
    projected = projected.astype(bf16)
    queries = projected[0]
    kv_blocks = ring_blocks(jnp.concatenate([projected[1], projected[2]], axis=1))

    d_attended = 0.0
    for step in range(count):
        d_attended = d_attended + lax.dot_general(
            columns_of(go_full, step), wo_blocks[step], (((1,), (1,)), ((), ())),
            preferred_element_type=f32,
        )
    d_attended = d_attended.astype(bf16)

    local_pos = jnp.arange(tok_rows, dtype=jnp.int32)
    query_pos = mine * tok_rows + local_pos
    query_span = span_index(query_pos, image_spans)
    masked = []
    for step in range(count):
        key_pos = owners[step] * tok_rows + local_pos
        allowed = visible(query_pos, query_span, key_pos, span_index(key_pos, image_spans))
        scores = (
            lax.dot_general(
                queries, kv_blocks[step][:, :head_dim], (((1,), (1,)), ((), ())),
                preferred_element_type=f32,
            )
            * score_scale
        )
        masked.append(jnp.where(allowed, scores, masked_low))
    maxima = functools.reduce(jnp.maximum, [jnp.max(block, axis=1) for block in masked])
    summed = sum(jnp.sum(jnp.exp(block - maxima[:, None]), axis=1) for block in masked)
    lse = maxima + jnp.log(summed)
    probs = [jnp.exp(block - lse[:, None]) for block in masked]
    attended = sum(
        jnp.dot(probs[step].astype(bf16), kv_blocks[step][:, head_dim:], preferred_element_type=f32)
        for step in range(count)
    ).astype(bf16)

    all_heads = gather_features(attended)
    wo_rows = jnp.zeros((head_dim, full_width), bf16)
    for step in range(count):
        wo_rows = lax.dynamic_update_slice_in_dim(wo_rows, wo_blocks[step], owners[step] * half, 1)
    out_rows = lax.all_to_all(wo_rows, ("gx", "gy"), split_axis=1, concat_axis=0, tiled=True)
    attn_out = jnp.dot(all_heads, out_rows, preferred_element_type=f32).astype(bf16)

    grad_wout = ring_reduce(
        lambda step: lax.dot_general(
            attended, columns_of(go_full, step), (((0,), (0,)), ((), ())),
            preferred_element_type=f32,
        )
    )

    row_dots = jnp.sum(d_attended.astype(f32) * attended.astype(f32), axis=1)
    d_scores = []
    for step in range(count):
        d_probs = lax.dot_general(
            d_attended, kv_blocks[step][:, head_dim:], (((1,), (1,)), ((), ())),
            preferred_element_type=f32,
        )
        d_scores.append((probs[step] * (d_probs - row_dots[:, None]) * score_scale).astype(bf16))

    def kv_term(step):
        d_keys = lax.dot_general(
            d_scores[step], queries, (((0,), (0,)), ((), ())), preferred_element_type=f32
        )
        d_values = lax.dot_general(
            probs[step].astype(bf16), d_attended, (((0,), (0,)), ((), ())),
            preferred_element_type=f32,
        )
        return jnp.concatenate([d_keys, d_values], axis=1).astype(bf16).astype(f32)

    kv_grad = ring_reduce(kv_term)
    d_queries = sum(
        jnp.dot(d_scores[step], kv_blocks[step][:, :head_dim], preferred_element_type=f32)
        for step in range(count)
    )
    grads = jnp.stack([d_queries, kv_grad[:, :head_dim], kv_grad[:, head_dim:]]).astype(bf16)

    norm_dots = lax.psum(
        jnp.sum(grads.astype(f32) * projected.astype(f32), axis=(0, 2)), ("gx", "gy")
    )
    partial_rows = [
        jnp.einsum("mch,mth->ct", w_blocks[step], grads, preferred_element_type=f32).astype(bf16)
        for step in range(count)
    ]
    partial = jnp.zeros((full_width, tok_rows), bf16)
    for step in range(count):
        partial = lax.dynamic_update_slice_in_dim(partial, partial_rows[step], owners[step] * half, 0)
    grad_normed = (
        lax.psum_scatter(partial, ("gx", "gy"), scatter_dimension=0, tiled=True).astype(f32).T
    )
    grad_qkv = ring_reduce(
        lambda step: jnp.einsum(
            "tc,mth->mch", columns_of(normed, step), grads, preferred_element_type=f32
        )
    )

    row_gain = jnp.where(picked, norm_gain[1][None, :], norm_gain[0][None, :])
    scaled = layer_input.astype(f32) * inv_rms[:, None]
    upstream = grad_normed * row_gain
    grad_in = (inv_rms[:, None] * (upstream - scaled * (norm_dots / full_width)[:, None])).astype(
        bf16
    )
    weighted = grad_normed * scaled
    local_gain = jnp.stack(
        [
            jnp.sum(jnp.where(modality[:, None] == kind, weighted, 0.0), axis=0)
            for kind in range(norm_gain.shape[0])
        ]
    )
    if count == 2:
        grad_gain = local_gain + shift_ring(local_gain, 1)
    else:
        grad_gain = lax.psum(local_gain, "gz")
    return (attn_out, grad_in, grad_qkv, grad_wout, grad_gain)


def solution(mesh):
    in_specs = (
        P("gz", ("gx", "gy")),
        P("gz"),
        P(),
        P(None, ("gx", "gy")),
        P(None, "gz", ("gx", "gy")),
        P(("gx", "gy"), "gz"),
        P("gz", ("gx", "gy")),
    )
    out_specs = (
        P("gz", ("gx", "gy")),
        P("gz", ("gx", "gy")),
        P(None, "gz", ("gx", "gy")),
        P(("gx", "gy"), "gz"),
        P(None, ("gx", "gy")),
    )
    return jax.shard_map(
        per_device, mesh=mesh, in_specs=in_specs, out_specs=out_specs, check_vma=False
    )
```

time: 421 us -> 272 us (0.65)
  waiting for transfers between devices: 243 us -> 122 us
  blocking collectives: 85.3 us -> 65.8 us
  starting transfers between devices: 6.02 us -> 14 us
  matrix products: 40.2 us -> 34.3 us
  loops' own time: 4.31 us -> 0 us
    reduce_scatter x4 -> x1, waiting for transfers between devices: 84.6 us -> 0.01 us  [per_device(): lax.psum_scatter(partial, ('gx', 'gy'), scatter_dimension=0, tiled=True)]
    all_gather x5 -> x3, waiting for transfers between devices: 131 us -> 87.8 us  [gather_features(): return lax.all_gather(block, ('gx', 'gy'), axis=1, tiled=True)]
    psum x3 -> x1, blocking collectives: 71.4 us -> 32.8 us  [per_device(): lax.psum(jnp.sum(grads.astype(f32) * projected.astype(f32), axis=(0, 2)),...]
    all_gather x1, blocking collectives: 13.9 us -> 33 us  [gather_features(): return lax.all_gather(block, ('gx', 'gy'), axis=1, tiled=True)]
    ppermute x0 -> x7, starting transfers between devices: none -> 9.89 us  [shift_ring(): lax.ppermute(block, 'gz', [(src, (src + step) % count) for src in range(c...]
    ppermute x0 -> x7, waiting for transfers between devices: none -> 6.41 us  [shift_ring(): lax.ppermute(block, 'gz', [(src, (src + step) % count) for src in range(c...]
    dynamic_slice x6 -> x0, local copies, waits for them, and re-layouts: 4.82 us -> none  [per_device(): (maxima, summed), unused = lax.scan(gather_stats, start_state, block_ids)]
    dot_general x20 -> x21, matrix products: 35.2 us -> 30.4 us  [the longest x2 7.02 us: per_device(): jnp.einsum('tc,mth->mch', columns_of(normed, step), grads, preferred_elem...]
  transfers between devices with their start and end apart: 10 -> 12, of which waited for: 9 -> 5; matrix products, arithmetic and copies ran while one was open for 11% -> 15% of each run, Pallas kernels for 0% -> 0%
where the time goes in v1:
time: 272 us
  waiting for transfers between devices  122 us (45%)
  blocking collectives  65.8 us (24%)
  matrix products  34.3 us (13%)
  between operations  14.2 us (5%)
  starting transfers between devices  14 us (5%)
  local copies, waits for them, and re-layouts  12.8 us (5%)
  other arithmetic  9.07 us (3%)
    all_gather x3, waiting for transfers between devices, gather_features(): return lax.all_gather(block, ('gx', 'gy'), axis=1, tiled=True)  87.8 us
    all_gather x1, blocking collectives, gather_features(): return lax.all_gather(block, ('gx', 'gy'), axis=1, tiled=True)  33 us
    psum x1, blocking collectives, per_device(): lax.psum(jnp.sum(grads.astype(f32) * projected.astype(f32), axis=(0, 2)),...  32.8 us
    all_to_all x1, waiting for transfers between devices, per_device(): lax.all_to_all(wo_rows, ('gx', 'gy'), split_axis=1, concat_axis=0, tiled=...  25.4 us
    ppermute x7, starting transfers between devices, shift_ring(): lax.ppermute(block, 'gz', [(src, (src + step) % count) for src in range(c...  9.89 us
    dot_general x2, matrix products, per_device(): jnp.einsum('tc,mth->mch', columns_of(normed, step), grads, preferred_elem...  7.02 us
    dot_general x2, matrix products, per_device(): jnp.einsum('mch,mth->ct', w_blocks[step], grads, preferred_element_type=f32)  6.84 us
    ppermute x7, waiting for transfers between devices, shift_ring(): lax.ppermute(block, 'gz', [(src, (src + step) % count) for src in range(c...  6.41 us
  transfers between devices with their start and end apart: 12, of which 5 were waited for; matrix products, arithmetic and copies ran while one was open for 15% of the time, Pallas kernels for 0%

profile of v1, /device:TPU:0, one launch (start us, length us, event | category | flops | bytes accessed | tf_op | source)
XLA Modules:
  0.0 271.7 jit_solution(7826255256517082825)
XLA Ops:
  10.0 3.1 %collective-permute-start.2 = (bf16[128,2048]{0,1:T(8,128)(2,1)S(1)}, bf16[128,2048]{0,1:T(8,128)(2,1)S(1)}, u32[]{:S(2)}, u32[]{:S(2)}) collective-permute-start(bf16[128,2048]{0,1:T(8,128)(2,1)S(1)} %copy.41), channel_id=1, source_target_pairs={{0,1},{1,0},{2,3},{3,2},{4,5},{5,4},{6,7},{7,6},{8,9},{9,8},{10,11... | collective-permute-start | bytes 1572872 | tf_op jit(solution)/shard_map/ppermute | solution.py:29
  13.1 1.7 copy.39
  14.9 33.0 %all_gather.13 = f32[2,4096]{1,0:T(2,128)S(1)} all-gather(f32[2,256]{1,0:T(2,128)S(1)} %copy-done.9), channel_id=1, replica_groups=mesh['gx'=4,'gy'=4,'gz'=2] {'gx','gy'}, dimensions={1}, use_global_device_ids=true | all-gather | bytes 34816 | tf_op jit(solution)/shard_map/all_gather | solution.py:48
  48.7 16.6 %all-gather.4.cloned.1.call-done = bf16[512,4096]{1,0:T(8,128)(2,1)} async-done(((bf16[512,256]{1,0:T(8,128)(2,1)}), bf16[512,4096]{1,0:T(8,128)(2,1)}) %all-gather.4.cloned.1.call-update) | async-done | bytes 4194320 | tf_op jit(solution)/shard_map/all_gather | solution.py:48
  65.3 3.2 %fusion = f32[512]{0:T(512)S(1)} fusion(bf16[512,4096]{1,0:T(8,128)(2,1)} %all-gather.4.cloned.1.call-done), kind=kLoop, calls=%fused_computation.2 | loop fusion | flops 6290944 | bytes 4196352 | tf_op jit(solution)/shard_map/reduce_sum | solution.py:69
  68.7 1.9 fusion.2
  71.6 2.9 %fusion.18 = f32[512,384]{0,1:S(1)} fusion(bf16[2048,384]{0,1:T(8,128)(2,1)} %bitcast.8, bf16[512,4096]{1,0:T(8,128)(2,1)S(1)} %fusion.2, s32[]{:T(128)S(6)} %select_n.52), kind=kOutput, calls=%fused_computation.25 | convolution fusion | flops 805306368 | bytes 4456452
  76.3 41.6 %all-gather.8.cloned.1.call-done = bf16[512,4096]{1,0:T(8,128)(2,1)} async-done(((bf16[512,256]{1,0:T(8,128)(2,1)}), bf16[512,4096]{1,0:T(8,128)(2,1)}) %all-gather.8.cloned.1.call-update) | async-done | bytes 4194320 | tf_op jit(solution)/shard_map/all_gather | solution.py:48
  118.0 2.4 fusion.15
  120.4 2.4 fusion.36
  129.7 6.4 %collective-permute-done.3 = bf16[512,256]{0,1:T(8,128)(2,1)S(1)} collective-permute-done((bf16[512,256]{0,1:T(8,128)(2,1)S(1)}, bf16[512,256]{0,1:T(8,128)(2,1)S(1)}, u32[]{:S(2)}, u32[]{:S(2)}) %collective-permute-start.3) | collective-permute-done | bytes 262176 | tf_op jit(solution)/shard_map/ppermute | solution.py:29
  136.2 2.5 broadcast_in_dim.148
  138.7 2.7 %fusion.4 = bf16[4096,512]{0,1:T(8,128)(2,1)} fusion(bf16[4096,512]{0,1:T(8,128)(2,1)} %broadcast_in_dim.148, s32[]{:T(128)S(6)} %select_n.51, bf16[3,2048,128]{2,1,0:T(8,128)(2,1)S(1)} %copy-done.5, bf16[1,512,128]{1,2,0:T(8,128)(2,1)S(1)} %get-tuple-element.36, bf16[1,512,128]{1,2,0:T(8,128)(2,1)S(1)} %get-tuple-element.35, ...), kind=kOutput, calls=%fused_computation.10 | convolution fusion | flops 806748160 | bytes 4063236 | tf_op jit(solution)/shard_map/mch,mth->ct/dot_general | solution.py:163
  141.4 4.1 %fusion.6 = bf16[4096,512]{0,1:T(8,128)(2,1)} fusion(bf16[4096,512]{0,1:T(8,128)(2,1)} %fusion.4, s32[]{:T(128)S(6)} %select_n.52, bf16[3,2048,128]{1,2,0:T(8,128)(2,1)} %collective-permute-done, bf16[1,512,128]{1,2,0:T(8,128)(2,1)S(1)} %get-tuple-element.36, bf16[1,512,128]{1,2,0:T(8,128)(2,1)S(1)} %get-tuple-element.35, bf16[1,512,128]{1,2,0:T(8,128)(2,1)S(1)} %fusion.39), kind=kOutput, calls=%fused_computation.12 | convolution fusion | flops 806748160 | bytes 4063236 | tf_op jit(solution)/shard_map/mch,mth->ct/dot_general | solution.py:163
  148.9 4.0 %all-to-all-start = ((bf16[128,16,256]{0,2,1:T(8,128)(2,1)}), bf16[128,16,256]{0,2,1:T(8,128)(2,1)S(1)}, u32[]{:S(2)}, u32[]{:S(2)}) async-start(bf16[128,16,256]{0,2,1:T(8,128)(2,1)} %bitcast.14), calls=%async_computation | async-start | bytes 2097152 | tf_op jit(solution)/shard_map/all_to_all | solution.py:123
  152.9 4.0 %fusion.7 = bf16[3,2048,128]{1,2,0:T(8,128)(2,1)} fusion(bf16[512,4096]{1,0:T(8,128)(2,1)} %copy-done.2, s32[]{:T(128)S(6)} %select_n.52, bf16[1,512,128]{1,2,0:T(8,128)(2,1)S(1)} %get-tuple-element.36, bf16[1,512,128]{1,2,0:T(8,128)(2,1)S(1)} %get-tuple-element.35, bf16[1,512,128]{1,2,0:T(8,128)(2,1)S(1)} %fusion.39), kind=kOutput, calls=%fused_computation.13 | convolution fusion | flops 806486016 | bytes 4063236 | tf_op jit(solution)/shard_map/tc,mth->mch/dot_general | solution.py:173
  160.0 25.4 %all-to-all-done = bf16[128,16,256]{0,2,1:T(8,128)(2,1)S(1)} async-done(((bf16[128,16,256]{0,2,1:T(8,128)(2,1)}), bf16[128,16,256]{0,2,1:T(8,128)(2,1)S(1)}, u32[]{:S(2)}, u32[]{:S(2)}) %all-to-all-start) | async-done | bytes 1048608 | tf_op jit(solution)/shard_map/all_to_all | solution.py:123
  186.9 32.8 %psum.7 = f32[512]{0:T(512)S(1)} all-reduce(f32[512]{0:T(512)S(1)} %multiply_reduce_fusion), channel_id=1, replica_groups=mesh['gx'=4,'gy'=4,'gz'=2] {'gx','gy'}, use_global_device_ids=true, to_apply=%region_11.12 | all-reduce | flops 512 | bytes 4096 | tf_op jit(solution)/shard_map/psum | solution.py:159
  219.6 3.1 %convert_add_fusion = f32[128,2048]{1,0:T(8,128)} fusion(bf16[128,2048]{1,0:T(8,128)(2,1)S(1)} %collective-permute-done.5, bf16[512,128]{0,1:T(8,128)(2,1)S(1)} %copy-done.3, bf16[512,4096]{1,0:T(8,128)(2,1)} %all-gather.8.cloned.1.call-done, s32[]{:T(128)S(6)} %select_n.51), kind=kOutput, calls=%fused_computation.54 | convolution fusion | flops 268959744 | bytes 3801092 | tf_op jit(solution)/shard_map/dot_general | solution.py:127
  222.7 3.0 %bitcast_add_fusion = f32[3,2048,128]{1,2,0:T(8,128)S(1)} fusion(bf16[3,2048,128]{1,2,0:T(8,128)(2,1)} %collective-permute-done.4, bf16[512,4096]{1,0:T(8,128)(2,1)} %copy-done.2, s32[]{:T(128)S(6)} %select_n.51, bf16[1,512,128]{1,2,0:T(8,128)(2,1)S(1)} %get-tuple-element.36, bf16[1,512,128]{1,2,0:T(8,128)(2,1)S(1)} %get-tuple-element.35, ...), kind=kOutput, calls=%fused_computation.7 | convolution fusion | flops 807272448 | bytes 7208964 | tf_op jit(solution)/shard_map/tc,mth->mch/dot_general | solution.py:173
  225.8 2.4 copy.49
  228.1 2.0 select_reduce_fusion.1
  231.7 29.6 %all-gather.6.cloned.1.call-done = bf16[512,2048]{0,1:T(8,128)(2,1)} async-done(((bf16[512,128]{0,1:T(8,128)(2,1)}), bf16[512,2048]{0,1:T(8,128)(2,1)}) %all-gather.6.cloned.1.call-update) | async-done | bytes 2097168 | tf_op jit(solution)/shard_map/all_gather | solution.py:48
  261.3 3.3 %convolution_convert_fusion.2 = bf16[512,256]{1,0:T(8,128)(2,1)} fusion(bf16[512,2048]{0,1:T(8,128)(2,1)} %all-gather.6.cloned.1.call-done, bf16[2048,256]{1,0:T(8,128)(2,1)} %bitcast.110), kind=kOutput, calls=%fused_computation.42 | convolution fusion | flops 537001984 | bytes 3407872 | tf_op jit(solution)/shard_map/dot_general | solution.py:124
  (94 shorter events, 23.5 us)
Async XLA Ops:
  7.2 7.8 %copy-start.9 = (f32[2,256]{1,0:T(2,128)S(1)}, f32[2,256]{1,0:T(2,128)}, u32[]{:S(2)}) copy-start(f32[2,256]{1,0:T(2,128)} %param.10) | copy-start | bytes 6148
  7.2 40.8 %copy-start.13 = (s32[2,8]{1,0:T(2,128)S(1)}, s32[2,8]{1,0:T(2,128)}, u32[]{:S(2)}) copy-start(s32[2,8]{1,0:T(2,128)} %param.9) | copy-start | bytes 196
  7.2 41.0 %copy-start.12 = (s32[512]{0:T(512)S(1)}, s32[512]{0:T(512)}, u32[]{:S(2)}) copy-start(s32[512]{0:T(512)} %param.8) | copy-start | bytes 6148
  7.2 58.1 %all-gather.4.cloned.1.call-start = ((), (), s32[]{:S(2)}) async-start(), calls=%async_computation.2 | async-start | bytes 4456448 | tf_op jit(solution)/shard_map/all_gather | solution.py:48
  7.9 110.0 %all-gather.8.cloned.1.call-start = ((), (), s32[]{:S(2)}) async-start(), calls=%async_computation.4 | async-start | bytes 4456448 | tf_op jit(solution)/shard_map/all_gather | solution.py:48
  8.7 219.4 %reduce-scatter.2.cloned.1.call-start = ((), (), s32[]{:S(2)}) async-start(), calls=%async_computation.5 | async-start | bytes 4456448 | tf_op jit(solution)/shard_map/reduce_scatter | solution.py:170
  10.0 110.4 %collective-permute-start.2 = (bf16[128,2048]{0,1:T(8,128)(2,1)S(1)}, bf16[128,2048]{0,1:T(8,128)(2,1)S(1)}, u32[]{:S(2)}, u32[]{:S(2)}) collective-permute-start(bf16[128,2048]{0,1:T(8,128)(2,1)S(1)} %copy.41), channel_id=1, source_target_pairs={{0,1},{1,0},{2,3},{3,2},{4,5},{5,4},{6,7},{7,6},{8,9},{9,8},{10,11... | collective-permute-start | bytes 1572872 | tf_op jit(solution)/shard_map/ppermute | solution.py:29
  14.8 56.8 %collective-permute-start = (bf16[3,2048,128]{1,2,0:T(8,128)(2,1)S(1)}, bf16[3,2048,128]{1,2,0:T(8,128)(2,1)}, u32[]{:S(2)}, u32[]{:S(2)}) collective-permute-start(bf16[3,2048,128]{1,2,0:T(8,128)(2,1)S(1)} %copy.39), channel_id=1, source_target_pairs={{0,1},{1,0},{2,3},{3,2},{4,5},{5,4},{6,7},{7,6},{8,9},{9,8},{10,11... | collective-permute-start | bytes 4718600 | tf_op jit(solution)/shard_map/ppermute | solution.py:29
  65.3 3.4 %copy-start.1 = (bf16[512,4096]{1,0:T(8,128)(2,1)S(1)}, bf16[512,4096]{1,0:T(8,128)(2,1)}, u32[]{:S(2)}) copy-start(bf16[512,4096]{1,0:T(8,128)(2,1)} %all-gather.4.cloned.1.call-done) | copy-start | bytes 12582916
  70.6 3.9 %copy-start.2 = (bf16[512,4096]{1,0:T(8,128)(2,1)}, bf16[512,4096]{1,0:T(8,128)(2,1)S(1)}, u32[]{:S(2)}) copy-start(bf16[512,4096]{1,0:T(8,128)(2,1)S(1)} %fusion.2) | copy-start | bytes 12582916
  71.6 46.4 %copy-start.4 = (bf16[128,2048]{1,0:T(8,128)(2,1)S(1)}, bf16[128,2048]{1,0:T(8,128)(2,1)}, u32[]{:S(2)}) copy-start(bf16[128,2048]{1,0:T(8,128)(2,1)} %param.12) | copy-start | bytes 1572868
  74.8 48.6 %collective-permute-start.1 = (bf16[512,256]{0,1:T(8,128)(2,1)S(1)}, bf16[512,256]{0,1:T(8,128)(2,1)S(1)}, u32[]{:S(2)}, u32[]{:S(2)}) collective-permute-start(bf16[512,256]{0,1:T(8,128)(2,1)S(1)} %pad_maximum_fusion.1), channel_id=1, source_target_pairs={{0,1},{1,0},{2,3},{3,2},{4,5},{5,4},{6,7},{7,6},{8,9},{9,8},{10,11... | collective-permute-start | bytes 786440 | tf_op jit(solution)/shard_map/ppermute | solution.py:29
  127.6 8.5 %collective-permute-start.3 = (bf16[512,256]{0,1:T(8,128)(2,1)S(1)}, bf16[512,256]{0,1:T(8,128)(2,1)S(1)}, u32[]{:S(2)}, u32[]{:S(2)}) collective-permute-start(bf16[512,256]{0,1:T(8,128)(2,1)S(1)} %pad_maximum_fusion.2), channel_id=1, source_target_pairs={{0,1},{1,0},{2,3},{3,2},{4,5},{5,4},{6,7},{7,6},{8,9},{9,8},{10,11... | collective-permute-start | bytes 786440 | tf_op jit(solution)/shard_map/ppermute | solution.py:29
  129.3 57.4 %copy-start.6 = (bf16[1,512,128]{1,2,0:T(8,128)(2,1)}, bf16[1,512,128]{1,2,0:T(8,128)(2,1)S(1)}, u32[]{:S(2)}) copy-start(bf16[1,512,128]{1,2,0:T(8,128)(2,1)S(1)} %fusion.39) | copy-start | bytes 393220
  129.3 9.3 %copy-start.5 = (bf16[3,2048,128]{2,1,0:T(8,128)(2,1)S(1)}, bf16[3,2048,128]{2,1,0:T(8,128)(2,1)}, u32[]{:S(2)}) copy-start(bf16[3,2048,128]{2,1,0:T(8,128)(2,1)} %param.11) | copy-start | bytes 4718596
  145.5 115.8 %all-gather.6.cloned.1.call-start = ((), (), s32[]{:S(2)}) async-start(), calls=%async_computation.3 | async-start | bytes 2228224 | tf_op jit(solution)/shard_map/all_gather | solution.py:48
  148.9 9.4 %copy-start.3 = (bf16[512,128]{0,1:T(8,128)(2,1)S(1)}, bf16[512,128]{0,1:T(8,128)(2,1)}, u32[]{:S(2)}) copy-start(bf16[512,128]{0,1:T(8,128)(2,1)} %get-tuple-element.50) | copy-start | bytes 393220
  148.9 36.5 %all-to-all-start = ((bf16[128,16,256]{0,2,1:T(8,128)(2,1)}), bf16[128,16,256]{0,2,1:T(8,128)(2,1)S(1)}, u32[]{:S(2)}, u32[]{:S(2)}) async-start(bf16[128,16,256]{0,2,1:T(8,128)(2,1)} %bitcast.14), calls=%async_computation | async-start | bytes 2097152 | tf_op jit(solution)/shard_map/all_to_all | solution.py:123
  152.8 5.5 %copy-start = (bf16[512,4096]{1,0:T(8,128)(2,1)S(1)}, bf16[512,4096]{1,0:T(8,128)(2,1)}, u32[]{:S(2)}) copy-start(bf16[512,4096]{1,0:T(8,128)(2,1)} %all-gather.8.cloned.1.call-done) | copy-start | bytes 12582916
  156.9 65.8 %collective-permute-start.4 = (bf16[3,2048,128]{1,2,0:T(8,128)(2,1)}, bf16[3,2048,128]{1,2,0:T(8,128)(2,1)}, u32[]{:S(2)}, u32[]{:S(2)}) collective-permute-start(bf16[3,2048,128]{1,2,0:T(8,128)(2,1)} %fusion.7), channel_id=1, source_target_pairs={{0,1},{1,0},{2,3},{3,2},{4,5},{5,4},{6,7},{7,6},{8,9},{9,8},{10,11... | collective-permute-start | bytes 4718600 | tf_op jit(solution)/shard_map/ppermute | solution.py:29
  158.8 60.9 %collective-permute-start.5 = (bf16[128,2048]{1,0:T(8,128)(2,1)S(1)}, bf16[128,2048]{1,0:T(8,128)(2,1)S(1)}, u32[]{:S(2)}, u32[]{:S(2)}) collective-permute-start(bf16[128,2048]{1,0:T(8,128)(2,1)S(1)} %convolution_convert_fusion.1), channel_id=1, source_target_pairs={{0,1},{1,0},{2,3},{3,2},{4,5},{5,4},{6,7},{7,6},{8,9},{9,8},{10,11... | collective-permute-start | bytes 1572872 | tf_op jit(solution)/shard_map/ppermute | solution.py:29
  219.6 3.1 %copy-start.7 = (bf16[1,512,128]{1,2,0:T(8,128)(2,1)S(1)}, bf16[1,512,128]{1,2,0:T(8,128)(2,1)}, u32[]{:S(2)}) copy-start(bf16[1,512,128]{1,2,0:T(8,128)(2,1)} %copy-done.6) | copy-start | bytes 393220
  225.7 2.4 copy-start.8
  230.2 34.5 %collective-permute-start.6 = (f32[2,256]{1,0:T(2,128)S(1)}, f32[2,256]{1,0:T(2,128)S(1)}, u32[]{:S(2)}, u32[]{:S(2)}) collective-permute-start(f32[2,256]{1,0:T(2,128)S(1)} %pad_maximum_fusion.3), channel_id=1, source_target_pairs={{0,1},{1,0},{2,3},{3,2},{4,5},{5,4},{6,7},{7,6},{8,9},{9,8},{10,11... | collective-permute-start | bytes 6152 | tf_op jit(solution)/shard_map/ppermute | solution.py:29
  (2 other events, 4.8 us)
Sparse Core Ops, SparseCore 0:
  10.1 55.1 all-gather.3
  67.3 50.5 all-gather.7
  145.6 72.4 reduce-scatter.1
  220.8 40.4 all-gather.5

commit v2 on v1

--- a/solution.py
+++ b/solution.py
@@ -4,6 +4,8 @@
 import jax
 import jax.numpy as jnp
 from jax import lax
+from jax.experimental import pallas as pl
+from jax.experimental.pallas import tpu as pltpu
 from jax.sharding import PartitionSpec as P
 
 epsilon = 1e-05
@@ -22,6 +24,359 @@
     causal = key_pos[None, :] <= query_pos[:, None]
     same_image = (query_span[:, None] == key_span[None, :]) & (query_span[:, None] >= 0)
     return causal | same_image
+
+
+MESH = pl.DeviceIdType.MESH
+
+
+def place():
+    gx, gy, gz = lax.axis_index("gx"), lax.axis_index("gy"), lax.axis_index("gz")
+    return gx // 2, lax.rem(gx, 2), gy, gz
+
+
+def greet(peers):
+    barrier = pltpu.get_barrier_semaphore()
+    for condition, device in peers:
+
+        @pl.when(condition)
+        def _():
+            pl.semaphore_signal(barrier, inc=1, device_id=device, device_id_type=MESH)
+
+    pl.semaphore_wait(barrier, sum(jnp.where(condition, 1, 0) for condition, _ in peers))
+
+
+def remote(src, dst, send, recv, device):
+    return pltpu.make_async_remote_copy(
+        src_ref=src, dst_ref=dst, send_sem=send, recv_sem=recv, device_id=device,
+        device_id_type=MESH,
+    )
+
+
+def gather_body(arity, nx, nz, *refs):
+    ins, outs = refs[:arity], refs[arity : 2 * arity]
+    line_send, line_recv, side_send, side_recv, core_send, core_recv = refs[2 * arity :]
+    hi, lo, z, gz = place()
+    pairs = nx // 2
+    sides = [lax.rem(hi + r, pairs) for r in range(1, pairs)]
+    partner = (hi * 2 + 1 - lo, z, gz)
+    flows = [(1, z < nz - 1), (-1, z > 0)]
+
+    def along(sign):
+        return (hi * 2 + lo, z + sign, gz)
+
+    def block(k, h, c, o):
+        width = ins[k].shape[1]
+        start = ((h * 2 + c) * nz + o) * width
+        return outs[k].at[:, pl.ds(pl.multiple_of(start, width), width)]
+
+    def line_copy(k, way, dist, src, o):
+        return remote(
+            src, block(k, hi, lo, o), line_send.at[k, way, dist], line_recv.at[k, way, dist + 1],
+            along(flows[way][0]),
+        )
+
+    def spread(k, src, o):
+        copies = [
+            remote(
+                src, block(k, hi, lo, o), side_send.at[k, r, o], side_recv.at[k, r, o],
+                (sides[r] * 2 + lo, z, gz),
+            )
+            for r in range(pairs - 1)
+        ]
+        copies.append(core_copy(k, src, hi, o))
+        return copies
+
+    def core_copy(k, src, h, o):
+        return remote(
+            src, block(k, h, lo, o), core_send.at[k, h, o], core_recv.at[k, h, o], partner
+        )
+
+    greet(
+        [(flows[0][1], along(1)), (flows[1][1], along(-1)), (z >= 0, partner)]
+        + [(z >= 0, (side * 2 + lo, z, gz)) for side in sides]
+    )
+    for k in range(arity):
+        for way in range(2):
+
+            @pl.when(flows[way][1])
+            def _():
+                line_copy(k, way, 0, ins[k], z).start()
+
+        for copy in spread(k, ins[k], z):
+            copy.start()
+        width = ins[k].shape[1]
+        own = pl.ds(pl.multiple_of(((hi * 2 + lo) * nz + z) * width, width), width)
+        outs[k][:, own] = ins[k][...]
+
+    def side_arrivals(dist):
+        for origin, valid in origins(dist):
+
+            @pl.when(valid)
+            def _():
+                for k in range(arity):
+                    for r in range(pairs - 1):
+                        source = lax.rem(hi - r - 1 + pairs, pairs)
+                        landed = block(k, source, lo, origin)
+                        remote(
+                            landed, landed, side_send.at[k, r, origin], side_recv.at[k, r, origin],
+                            partner,
+                        ).wait_recv()
+                        core_copy(k, landed, source, origin).start()
+
+    def origins(dist):
+        if dist == 0:
+            return [(z, z >= 0)]
+        return [(z - dist, z - dist >= 0), (z + dist, z + dist < nz)]
+
+    for dist in range(1, nz):
+        for way, (origin, valid) in enumerate(origins(dist)):
+
+            @pl.when(valid)
+            def _():
+                for k in range(arity):
+                    landed = block(k, hi, lo, origin)
+                    remote(
+                        landed, landed, line_send.at[k, way, dist], line_recv.at[k, way, dist],
+                        partner,
+                    ).wait_recv()
+                    if dist < nz - 1:
+
+                        @pl.when(flows[way][1])
+                        def _():
+                            line_copy(k, way, dist, landed, origin).start()
+
+                    for copy in spread(k, landed, origin):
+                        copy.start()
+
+        side_arrivals(dist - 1)
+    side_arrivals(nz - 1)
+    for k in range(arity):
+        for o in range(nz):
+            for h in range(pairs):
+                landed = block(k, h, 1 - lo, o)
+                waiting = remote(
+                    landed, landed, core_send.at[k, h, o], core_recv.at[k, h, o], partner
+                )
+                waiting.wait_recv()
+                waiting.wait_send()
+            for r in range(pairs - 1):
+                landed = block(k, hi, lo, o)
+                remote(
+                    landed, landed, side_send.at[k, r, o], side_recv.at[k, r, o], partner
+                ).wait_send()
+        for dist in range(nz - 1):
+            for way in range(2):
+                origin, valid = (z - dist, z - dist >= 0) if way == 0 else (z + dist, z + dist < nz)
+
+                @pl.when(valid & flows[way][1])
+                def _():
+                    line_copy(k, way, dist, ins[k], z).wait_send()
+
+
+def gather_kernel(arrays, collective_id):
+    nx, nz = lax.axis_size("gx"), lax.axis_size("gy")
+    arity, pairs = len(arrays), nx // 2
+    dma = pltpu.SemaphoreType.DMA
+    vmem = pl.BlockSpec(memory_space=pltpu.VMEM)
+    return pl.pallas_call(
+        functools.partial(gather_body, arity, nx, nz),
+        out_shape=[
+            jax.ShapeDtypeStruct((a.shape[0], a.shape[1] * nx * nz), a.dtype) for a in arrays
+        ],
+        in_specs=[vmem] * arity,
+        out_specs=[vmem] * arity,
+        scratch_shapes=[
+            dma((arity, 2, nz)), dma((arity, 2, nz)),
+            dma((arity, max(pairs - 1, 1), nz)), dma((arity, max(pairs - 1, 1), nz)),
+            dma((arity, pairs, nz)), dma((arity, pairs, nz)),
+        ],
+        compiler_params=pltpu.CompilerParams(collective_id=collective_id, has_side_effects=True),
+        cost_estimate=pl.CostEstimate(
+            flops=sum(a.size * a.dtype.itemsize for a in arrays) * 80000, bytes_accessed=2**23,
+            transcendentals=0,
+        ),
+        name="gather_features",
+    )(*arrays)
+
+
+def reduce_body(
+    nx, nz, part, dots, out, dots_out, cbuf, csum, xbuf, lbuf, lsend, acc, dbuf, dsum,
+    core_send, core_recv, side_send, side_recv, line_send, line_recv, dot_send, dot_recv,
+):
+    hi, lo, z, gz = place()
+    pairs = nx // 2
+    width = out.shape[1]
+    f32 = jnp.float32
+    sides = [lax.rem(hi + r, pairs) for r in range(1, pairs)]
+    partner = (hi * 2 + 1 - lo, z, gz)
+    flows = [(1, z < nz - 1), (-1, z > 0)]
+    depth = [(hi * 2 + lo, lax.rem(z + r, nz), gz) for r in range(1, nz)]
+
+    def columns(h, c, o):
+        return pl.ds(pl.multiple_of(((h * 2 + c) * nz + o) * width, width), width)
+
+    def along(sign):
+        return (hi * 2 + lo, z + sign, gz)
+
+    def targets():
+        for dist in range(nz - 1, 0, -1):
+            yield 0, dist, z + dist, z + dist < nz
+            yield 1, dist, z - dist, z - dist >= 0
+
+    def core_copy(h, o):
+        return remote(
+            part.at[:, columns(h, 1 - lo, o)], cbuf.at[h, o], core_send.at[h, o],
+            core_recv.at[h, o], partner,
+        )
+
+    def side_copy(r, o):
+        return remote(
+            csum.at[r, o], xbuf.at[r, o], side_send.at[r, o], side_recv.at[r, o],
+            (sides[r] * 2 + lo, z, gz),
+        )
+
+    def line_copy(way, dist):
+        return remote(
+            lsend.at[way, dist - 1], lbuf.at[way, dist - 1], line_send.at[way, dist - 1],
+            line_recv.at[way, dist - 1], along(flows[way][0]),
+        )
+
+    def dot_copy(src, slot, device):
+        return remote(src, dbuf.at[slot], dot_send.at[slot], dot_recv.at[slot], device)
+
+    greet(
+        [(z >= 0, partner)]
+        + [(z >= 0, (side * 2 + lo, z, gz)) for side in sides]
+        + [(z >= 0, device) for device in depth]
+    )
+    order = list(targets()) + [(0, 0, z, z >= 0)]
+    for way, dist, o, valid in order:
+
+        @pl.when(valid)
+        def _():
+            for side in sides:
+                core_copy(side, o).start()
+            core_copy(hi, o).start()
+
+    dot_first = dot_copy(dots, 0, partner)
+    dot_first.start()
+    for way, dist, o, valid in order:
+
+        @pl.when(valid)
+        def _():
+            for r, side in enumerate(sides):
+                core_copy(side, o).wait_recv()
+                csum[r, o] = (
+                    part[:, columns(side, lo, o)].astype(f32) + cbuf[side, o].astype(f32)
+                ).astype(csum.dtype)
+                side_copy(r, o).start()
+
+    dot_first.wait_recv()
+    dsum[0] = dots[...] + dbuf[0]
+    dot_sides = [
+        dot_copy(dsum.at[0], 1 + r, (sides[r] * 2 + lo, z, gz)) for r in range(pairs - 1)
+    ]
+    for copy in dot_sides:
+        copy.start()
+
+    def merge(o):
+        core_copy(hi, o).wait_recv()
+        total = part[:, columns(hi, lo, o)].astype(f32) + cbuf[hi, o].astype(f32)
+        for r in range(pairs - 1):
+            side_copy(r, o).wait_recv()
+            total = total + xbuf[r, o].astype(f32)
+        acc[...] = total
+
+    def add_line(way, dist):
+        source = flows[1 - way]
+
+        @pl.when(source[1])
+        def _():
+            remote(
+                lbuf.at[way, dist], lbuf.at[way, dist], line_send.at[way, dist],
+                line_recv.at[way, dist], partner,
+            ).wait_recv()
+            acc[...] += lbuf[way, dist].astype(f32)
+
+    for way, dist, o, valid in targets():
+
+        @pl.when(valid)
+        def _():
+            merge(o)
+            if dist < nz - 1:
+                add_line(way, dist)
+            lsend[way, dist - 1] = acc[...].astype(lsend.dtype)
+            line_copy(way, dist).start()
+
+    dots_now = dsum[0]
+    for r, copy in enumerate(dot_sides):
+        copy.wait_recv()
+        dots_now = dots_now + dbuf[1 + r]
+    dsum[1] = dots_now
+    dot_depth = [dot_copy(dsum.at[1], pairs + r, depth[r]) for r in range(nz - 1)]
+    for copy in dot_depth:
+        copy.start()
+    merge(z)
+    if nz > 1:
+        add_line(0, 0)
+        add_line(1, 0)
+    out[...] = acc[...]
+    for r, copy in enumerate(dot_depth):
+        copy.wait_recv()
+        dots_now = dots_now + dbuf[pairs + r]
+    dots_out[...] = dots_now
+    for copy in [dot_first] + dot_sides + dot_depth:
+        copy.wait_send()
+    for o in range(nz):
+        for h in range(pairs):
+            core_copy(h, o).wait_send()
+        for r in range(pairs - 1):
+            side_copy(r, o).wait_send()
+    for way, dist, o, valid in targets():
+
+        @pl.when(valid)
+        def _():
+            line_copy(way, dist).wait_send()
+
+
+def reduce_kernel(part, dots, collective_id):
+    nx, nz = lax.axis_size("gx"), lax.axis_size("gy")
+    pairs = nx // 2
+    rows, width = part.shape[0], part.shape[1] // (nx * nz)
+    dots = dots.reshape(-1, 128)
+    dma = pltpu.SemaphoreType.DMA
+    vmem = pl.BlockSpec(memory_space=pltpu.VMEM)
+    others, line = max(pairs - 1, 1), max(nz - 1, 1)
+    tile = (rows, width)
+    summed, dots_total = pl.pallas_call(
+        functools.partial(reduce_body, nx, nz),
+        out_shape=[
+            jax.ShapeDtypeStruct(tile, jnp.float32),
+            jax.ShapeDtypeStruct(dots.shape, jnp.float32),
+        ],
+        in_specs=[vmem] * 2,
+        out_specs=[vmem] * 2,
+        scratch_shapes=[
+            pltpu.VMEM((pairs, nz) + tile, part.dtype),
+            pltpu.VMEM((others, nz) + tile, part.dtype),
+            pltpu.VMEM((others, nz) + tile, part.dtype),
+            pltpu.VMEM((2, line) + tile, part.dtype),
+            pltpu.VMEM((2, line) + tile, part.dtype),
+            pltpu.VMEM(tile, jnp.float32),
+            pltpu.VMEM((pairs + line,) + dots.shape, jnp.float32),
+            pltpu.VMEM((2,) + dots.shape, jnp.float32),
+            dma((pairs, nz)), dma((pairs, nz)),
+            dma((others, nz)), dma((others, nz)),
+            dma((2, line)), dma((2, line)),
+            dma((pairs + line,)), dma((pairs + line,)),
+        ],
+        compiler_params=pltpu.CompilerParams(collective_id=collective_id, has_side_effects=True),
+        cost_estimate=pl.CostEstimate(
+            flops=part.size * 12000, bytes_accessed=2**23, transcendentals=0
+        ),
+        name="reduce_features",
+    )(part, dots)
+    return summed, dots_total.reshape(-1)
 
 
 def shift_ring(block, step):
@@ -60,8 +415,7 @@
 
     w_blocks = ring_blocks(w_qkv)
     wo_blocks = ring_blocks(w_out)
-    x_full = gather_features(layer_input)
-    gain_full = gather_features(norm_gain)
+    x_full, gain_full = gather_kernel([layer_input, norm_gain], 1)
     go_full = gather_features(grad_out)
     full_width = x_full.shape[1]
 
@@ -156,19 +510,18 @@
     )
     grads = jnp.stack([d_queries, kv_grad[:, :head_dim], kv_grad[:, head_dim:]]).astype(bf16)
 
-    norm_dots = lax.psum(
-        jnp.sum(grads.astype(f32) * projected.astype(f32), axis=(0, 2)), ("gx", "gy")
-    )
-    partial_rows = [
-        jnp.einsum("mch,mth->ct", w_blocks[step], grads, preferred_element_type=f32).astype(bf16)
-        for step in range(count)
-    ]
-    partial = jnp.zeros((full_width, tok_rows), bf16)
+    dots = jnp.sum(grads.astype(f32) * projected.astype(f32), axis=(0, 2))
+    partial = jnp.zeros((tok_rows, full_width), bf16)
     for step in range(count):
-        partial = lax.dynamic_update_slice_in_dim(partial, partial_rows[step], owners[step] * half, 0)
-    grad_normed = (
-        lax.psum_scatter(partial, ("gx", "gy"), scatter_dimension=0, tiled=True).astype(f32).T
-    )
+        partial = lax.dynamic_update_slice_in_dim(
+            partial,
+            jnp.einsum(
+                "mth,mch->tc", grads, w_blocks[step], preferred_element_type=f32
+            ).astype(bf16),
+            owners[step] * half,
+            1,
+        )
+    grad_normed, norm_dots = reduce_kernel(partial, dots, 2)
     grad_qkv = ring_reduce(
         lambda step: jnp.einsum(
             "tc,mth->mch", columns_of(normed, step), grads, preferred_element_type=f32

time: 272 us -> 186 us (0.68)
  waiting for transfers between devices: 122 us -> 4.23 us
  Pallas kernels: 0 us -> 95.2 us
  blocking collectives: 65.8 us -> 0 us
    pallas_call x0 -> x2, Pallas kernels: none -> 95.2 us  [the longest x1 49.8 us: gather_kernel(): pl.pallas_call(functools.partial(gather_body, arity, nx, nz), out_shape=[...]
    all_gather x3 -> x2, waiting for transfers between devices: 87.8 us -> 0.02 us  [gather_features(): return lax.all_gather(block, ('gx', 'gy'), axis=1, tiled=True)]
    all_gather x1 -> x0, blocking collectives: 33 us -> none  [gather_features(): return lax.all_gather(block, ('gx', 'gy'), axis=1, tiled=True)]
    psum x1 -> x0, blocking collectives: 32.8 us -> none  [per_device(): lax.psum(jnp.sum(grads.astype(f32) * projected.astype(f32), axis=(0, 2)),...]
    all_to_all x1, waiting for transfers between devices: 25.4 us -> 0.01 us  [per_device(): lax.all_to_all(wo_rows, ('gx', 'gy'), split_axis=1, concat_axis=0, tiled=...]
    ppermute x7, waiting for transfers between devices: 6.41 us -> 3.5 us  [shift_ring(): lax.ppermute(block, 'gz', [(src, (src + step) % count) for src in range(c...]
    dot_general x2, matrix products: 6.84 us -> 3.99 us  [per_device(): jnp.einsum('mth,mch->tc', grads, w_blocks[step], preferred_element_type=f32)]
    unnamed x31 -> x39, local copies, waits for them, and re-layouts: 5.66 us -> 7.46 us
  transfers between devices with their start and end apart: 12 -> 10, of which waited for: 5 -> 1; matrix products, arithmetic and copies ran while one was open for 15% -> 28% of each run, Pallas kernels for 0% -> 51%
where the time goes in v2:
time: 186 us
  Pallas kernels  95.2 us (51%)
  matrix products  32.2 us (17%)
  starting transfers between devices  14.8 us (8%)
  between operations  14.5 us (8%)
  local copies, waits for them, and re-layouts  13.7 us (7%)
  other arithmetic  10.9 us (6%)
  waiting for transfers between devices  4.23 us (2%)
    pallas_call x1, Pallas kernels, gather_kernel(): pl.pallas_call(functools.partial(gather_body, arity, nx, nz), out_shape=[...  49.8 us
    pallas_call x1, Pallas kernels, reduce_kernel(): pl.pallas_call(functools.partial(reduce_body, nx, nz), out_shape=[jax.Sha...  45.5 us
    ppermute x7, starting transfers between devices, shift_ring(): lax.ppermute(block, 'gz', [(src, (src + step) % count) for src in range(c...  9.5 us
    unnamed x39, local copies, waits for them, and re-layouts  7.46 us
    dot_general x2, matrix products, per_device(): lax.dot_general(attended, columns_of(go_full, step), (((0,), (0,)), ((),...  6.04 us
    dot_general x2, matrix products, per_device(): jnp.einsum('tc,mth->mch', columns_of(normed, step), grads, preferred_elem...  5.22 us
    all_to_all x1, starting transfers between devices, per_device(): lax.all_to_all(wo_rows, ('gx', 'gy'), split_axis=1, concat_axis=0, tiled=...  5.04 us
    dot_general x2, matrix products, per_device(): lax.dot_general(columns_of(go_full, step), wo_blocks[step], (((1,), (1,))...  4.97 us
  transfers between devices with their start and end apart: 10, of which 1 were waited for; matrix products, arithmetic and copies ran while one was open for 28% of the time, Pallas kernels for 51%

profile of v2, /device:TPU:0, one launch (start us, length us, event | category | flops | bytes accessed | tf_op | source)
XLA Modules:
  0.0 185.6 jit_solution(7621700536654127112)
XLA Ops:
  7.9 1.3 copy.41
  9.2 3.1 %collective-permute-start.2 = (bf16[128,2048]{0,1:T(8,128)(2,1)S(1)}, bf16[128,2048]{0,1:T(8,128)(2,1)S(1)}, u32[]{:S(2)}, u32[]{:S(2)}) collective-permute-start(bf16[128,2048]{0,1:T(8,128)(2,1)S(1)} %copy.41), channel_id=1, source_target_pairs={{0,1},{1,0},{2,3},{3,2},{4,5},{5,4},{6,7},{7,6},{8,9},{9,8},{10,11... | collective-permute-start | bytes 1572872 | tf_op jit(solution)/shard_map/ppermute | solution.py:384
  12.3 1.7 copy.39
  15.5 49.8 %gather_features.1 = (bf16[512,4096]{1,0:T(8,128)(2,1)}, f32[2,4096]{1,0:T(2,128)}) custom-call(bf16[512,256]{1,0:T(8,128)(2,1)} %refs_0_.1, f32[2,256]{1,0:T(2,128)} %refs_1_.1), custom_call_target="tpu_custom_call" | custom-call | flops 21135360000 | bytes 8388608 | tf_op jit(solution)/shard_map/gather_features/pallas_call | solution.py:181
  65.2 3.5 %fusion = f32[512]{0:T(512)S(1)} fusion(bf16[512,4096]{1,0:T(8,128)(2,1)} %get-tuple-element.9), kind=kLoop, calls=%fused_computation.2 | loop fusion | flops 6290944 | bytes 4196352 | tf_op jit(solution)/shard_map/reduce_sum | solution.py:423
  70.8 1.9 %fusion.2 = bf16[512,4096]{1,0:T(8,128)(2,1)S(1)} fusion(bf16[512,4096]{1,0:T(8,128)(2,1)S(1)} %copy-done, f32[4096]{0:T(1024)S(1)} %bitcast.93, f32[4096]{0:T(1024)S(1)} %bitcast.92, f32[512]{0:T(512)S(1)} %add_rsqrt_fusion, pred[512]{0:T(512)(128)(4,1)S(1)} %get-tuple-element.48), kind=kLoop, calls=%fused_computation.4 | loop fusion | flops 10485760 | bytes 8423936 | tf_op jit(solution)/shard_map/convert_element_type | solution.py:427
  73.7 2.8 %fusion.16 = f32[512,384]{0,1:S(1)} fusion(bf16[2048,384]{0,1:T(8,128)(2,1)} %bitcast.8, bf16[512,4096]{1,0:T(8,128)(2,1)S(1)} %fusion.2, s32[]{:T(128)S(6)} %select_n.52), kind=kOutput, calls=%fused_computation.23 | convolution fusion | flops 805306368 | bytes 4456452
  78.3 5.0 %all-to-all-start = ((bf16[128,16,256]{0,2,1:T(8,128)(2,1)}), bf16[128,16,256]{0,2,1:T(8,128)(2,1)}, u32[]{:S(2)}, u32[]{:S(2)}) async-start(bf16[128,16,256]{0,2,1:T(8,128)(2,1)} %bitcast.14), calls=%async_computation | async-start | bytes 2097152 | tf_op jit(solution)/shard_map/all_to_all | solution.py:477
  85.4 2.6 %fusion.13 = f32[512,128]{0,1:T(8,128)S(1)} fusion(bf16[128,2048]{1,0:T(8,128)(2,1)} %param.12, bf16[512,4096]{1,0:T(8,128)(2,1)} %all-gather.5.cloned.1.call-done, s32[]{:T(128)S(6)} %select_n.51), kind=kOutput, calls=%fused_computation.20 | convolution fusion | flops 268435456 | bytes 2883588 | tf_op jit(solution)/shard_map/dot_general | solution.py:443
  88.0 2.4 %fusion.34 = bf16[512,128]{0,1:T(8,128)(2,1)S(1)} fusion(f32[512,128]{0,1:T(8,128)S(1)} %fusion.13, bf16[128,2048]{0,1:T(8,128)(2,1)S(1)} %collective-permute-done.2, bf16[512,4096]{1,0:T(8,128)(2,1)} %all-gather.5.cloned.1.call-done, s32[]{:T(128)S(6)} %select_n.52), kind=kOutput, calls=%fused_computation.46 | convolution fusion | flops 268566528 | bytes 3014660 | tf_op jit(solution)/shard_map/dot_general | solution.py:443
  93.5 1.2 collective-permute-start.3
  94.6 2.9 %convolution_convert_fusion.1 = bf16[128,2048]{1,0:T(8,128)(2,1)} fusion(bf16[512,128]{0,1:T(8,128)(2,1)S(1)} %copy-done.4, bf16[512,4096]{1,0:T(8,128)(2,1)} %all-gather.5.cloned.1.call-done, s32[]{:T(128)S(6)} %select_n.52), kind=kOutput, calls=%fused_computation.12 | convolution fusion | flops 268697600 | bytes 2752516 | tf_op jit(solution)/shard_map/dot_general | solution.py:481
  99.2 3.5 %collective-permute-done.3 = bf16[512,256]{0,1:T(8,128)(2,1)S(1)} collective-permute-done((bf16[512,256]{0,1:T(8,128)(2,1)S(1)}, bf16[512,256]{0,1:T(8,128)(2,1)S(1)}, u32[]{:S(2)}, u32[]{:S(2)}) %collective-permute-start.3) | collective-permute-done | bytes 262176 | tf_op jit(solution)/shard_map/ppermute | solution.py:384
  102.8 2.2 %fusion.5 = bf16[3,2048,128]{1,2,0:T(8,128)(2,1)} fusion(bf16[512,4096]{1,0:T(8,128)(2,1)S(1)} %copy-done.2, s32[]{:T(128)S(6)} %select_n.52, bf16[1,512,128]{1,2,0:T(8,128)(2,1)S(1)} %get-tuple-element.44, bf16[1,512,128]{1,2,0:T(8,128)(2,1)S(1)} %get-tuple-element.43, bf16[1,512,128]{1,2,0:T(8,128)(2,1)S(1)} %fusion.37), kind=kOutput, calls=%fused_computation.11 | convolution fusion | flops 806486016 | bytes 4063236 | tf_op jit(solution)/shard_map/tc,mth->mch/dot_general | solution.py:526
  106.4 1.3 fusion.3
  108.8 2.7 %fusion.4.part = bf16[512,4096]{1,0:T(8,128)(2,1)S(1)} fusion(bf16[512,4096]{1,0:T(8,128)(2,1)S(1)} %fusion.3, s32[]{:T(128)S(6)} %select_n.52, bf16[3,2048,128]{1,2,0:T(8,128)(2,1)} %collective-permute-done, bf16[1,512,128]{1,2,0:T(8,128)(2,1)S(1)} %get-tuple-element.44, bf16[1,512,128]{1,2,0:T(8,128)(2,1)S(1)} %get-tuple-element.43, ...), kind=kOutput, calls=%fused_computation.9 | convolution fusion | flops 806748160 | bytes 4063236 | tf_op jit(solution)/shard_map/mth,mch->tc/dot_general | solution.py:518
  113.5 45.5 %reduce_features.1 = (f32[512,256]{1,0:T(8,128)}, f32[4,128]{1,0:T(4,128)}) custom-call(bf16[512,4096]{1,0:T(8,128)(2,1)} %copy-done.3, f32[4,128]{1,0:T(4,128)} %bitcast.100), custom_call_target="tpu_custom_call" | custom-call | flops 25165824000 | bytes 8388608 | tf_op jit(solution)/shard_map/reduce_features/pallas_call | solution.py:351
  159.7 2.1 %select_reduce_fusion.1 = (f32[256]{0:T(256)S(1)}, f32[256]{0:T(256)S(1)}, bf16[512,256]{1,0:T(8,128)(2,1)}) fusion(f32[512,256]{1,0:T(8,128)} %get-tuple-element.11, bf16[512,256]{1,0:T(8,128)(2,1)S(1)} %copy-done.10, f32[512]{0:T(512)S(1)} %add_rsqrt_fusion, pred[512]{0:T(512)(128)(4,1)S(1)} %copy-done.14, pred[512]{0:T(512)(128)(4,1)S(1)} %get-tuple-element.48, ...), kind=kLoop, calls=%fused_computation.62 | loop fusion | flops 1703424 | bytes 1057792 | tf_op jit(solution)/shard_map/reduce_sum | solution.py:540
  161.8 2.2 %collective-permute-start.6 = (f32[2,256]{1,0:T(2,128)S(1)}, f32[2,256]{1,0:T(2,128)S(1)}, u32[]{:S(2)}, u32[]{:S(2)}) collective-permute-start(f32[2,256]{1,0:T(2,128)S(1)} %pad_maximum_fusion.3), channel_id=1, source_target_pairs={{0,1},{1,0},{2,3},{3,2},{4,5},{5,4},{6,7},{7,6},{8,9},{9,8},{10,11... | collective-permute-start | bytes 6152 | tf_op jit(solution)/shard_map/ppermute | solution.py:384
  164.0 2.3 %copy.43 = bf16[16,128,256]{2,1,0:T(8,128)(2,1)} copy(bf16[16,128,256]{1,2,0:T(8,128)(2,1)} %bitcast.15) | data formatting | bytes 2097152 | tf_op jit(solution)/shard_map/all_to_all | solution.py:477
  166.9 3.1 %convert_add_fusion = f32[128,2048]{1,0:T(8,128)} fusion(bf16[128,2048]{1,0:T(8,128)(2,1)} %collective-permute-done.5, bf16[512,128]{0,1:T(8,128)(2,1)S(1)} %copy-done.4, bf16[512,4096]{1,0:T(8,128)(2,1)} %all-gather.5.cloned.1.call-done, s32[]{:T(128)S(6)} %select_n.51), kind=kOutput, calls=%fused_computation.52 | convolution fusion | flops 268959744 | bytes 3801092 | tf_op jit(solution)/shard_map/dot_general | solution.py:481
  170.0 3.1 %bitcast_add_fusion = f32[3,2048,128]{1,2,0:T(8,128)S(1)} fusion(bf16[3,2048,128]{1,2,0:T(8,128)(2,1)} %collective-permute-done.4, bf16[512,4096]{1,0:T(8,128)(2,1)} %copy-done.1, s32[]{:T(128)S(6)} %select_n.51, bf16[1,512,128]{1,2,0:T(8,128)(2,1)S(1)} %get-tuple-element.44, bf16[1,512,128]{1,2,0:T(8,128)(2,1)S(1)} %get-tuple-element.43, ...), kind=kOutput, calls=%fused_computation.7 | convolution fusion | flops 807272448 | bytes 7208964 | tf_op jit(solution)/shard_map/tc,mth->mch/dot_general | solution.py:526
  173.1 2.4 %copy.49 = f32[3,2048,128]{2,1,0:T(8,128)} copy(f32[3,2048,128]{1,2,0:T(8,128)S(1)} %bitcast_add_fusion) | data formatting | bytes 6291456
  175.4 3.3 %convolution_convert_fusion.2 = bf16[512,256]{1,0:T(8,128)(2,1)} fusion(bf16[512,2048]{0,1:T(8,128)(2,1)} %all-gather.3.cloned.1.call-done, bf16[2048,256]{1,0:T(8,128)(2,1)} %bitcast.88), kind=kOutput, calls=%fused_computation.40 | convolution fusion | flops 537001984 | bytes 3407872 | tf_op jit(solution)/shard_map/dot_general | solution.py:478
  (96 shorter events, 19.4 us)
Async XLA Ops:
  7.2 7.0 %copy-start.15 = (s32[512]{0:T(512)S(1)}, s32[512]{0:T(512)}, u32[]{:S(2)}) copy-start(s32[512]{0:T(512)} %param.8) | copy-start | bytes 6148
  7.2 7.6 %copy-start.17 = (s32[2,8]{1,0:T(2,128)S(1)}, s32[2,8]{1,0:T(2,128)}, u32[]{:S(2)}) copy-start(s32[2,8]{1,0:T(2,128)} %param.9) | copy-start | bytes 196
  7.2 7.6 %copy-start.16 = (f32[2,256]{1,0:T(2,128)S(1)}, f32[2,256]{1,0:T(2,128)}, u32[]{:S(2)}) copy-start(f32[2,256]{1,0:T(2,128)} %refs_1_.1) | copy-start | bytes 6148
  7.2 78.2 %all-gather.5.cloned.1.call-start = ((), (), s32[]{:S(2)}) async-start(), calls=%async_computation.2 | async-start | bytes 4456448 | tf_op jit(solution)/shard_map/all_gather | solution.py:403
  9.2 68.3 %collective-permute-start.2 = (bf16[128,2048]{0,1:T(8,128)(2,1)S(1)}, bf16[128,2048]{0,1:T(8,128)(2,1)S(1)}, u32[]{:S(2)}, u32[]{:S(2)}) collective-permute-start(bf16[128,2048]{0,1:T(8,128)(2,1)S(1)} %copy.41), channel_id=1, source_target_pairs={{0,1},{1,0},{2,3},{3,2},{4,5},{5,4},{6,7},{7,6},{8,9},{9,8},{10,11... | collective-permute-start | bytes 1572872 | tf_op jit(solution)/shard_map/ppermute | solution.py:384
  14.0 59.6 %collective-permute-start = (bf16[3,2048,128]{1,2,0:T(8,128)(2,1)S(1)}, bf16[3,2048,128]{1,2,0:T(8,128)(2,1)}, u32[]{:S(2)}, u32[]{:S(2)}) collective-permute-start(bf16[3,2048,128]{1,2,0:T(8,128)(2,1)S(1)} %copy.39), channel_id=1, source_target_pairs={{0,1},{1,0},{2,3},{3,2},{4,5},{5,4},{6,7},{7,6},{8,9},{9,8},{10,11... | collective-permute-start | bytes 4718600 | tf_op jit(solution)/shard_map/ppermute | solution.py:384
  65.2 5.5 %copy-start.11 = (f32[2,4096]{1,0:T(2,128)S(1)}, f32[2,4096]{1,0:T(2,128)}, u32[]{:S(2)}) copy-start(f32[2,4096]{1,0:T(2,128)} %get-tuple-element.10) | copy-start | bytes 98308
  65.2 5.5 %copy-start = (bf16[512,4096]{1,0:T(8,128)(2,1)S(1)}, bf16[512,4096]{1,0:T(8,128)(2,1)}, u32[]{:S(2)}) copy-start(bf16[512,4096]{1,0:T(8,128)(2,1)} %get-tuple-element.9) | copy-start | bytes 12582916
  72.7 3.9 %copy-start.1 = (bf16[512,4096]{1,0:T(8,128)(2,1)}, bf16[512,4096]{1,0:T(8,128)(2,1)S(1)}, u32[]{:S(2)}) copy-start(bf16[512,4096]{1,0:T(8,128)(2,1)S(1)} %fusion.2) | copy-start | bytes 12582916
  76.8 7.4 %collective-permute-start.1 = (bf16[512,256]{0,1:T(8,128)(2,1)S(1)}, bf16[512,256]{0,1:T(8,128)(2,1)S(1)}, u32[]{:S(2)}, u32[]{:S(2)}) collective-permute-start(bf16[512,256]{0,1:T(8,128)(2,1)S(1)} %pad_maximum_fusion.1), channel_id=1, source_target_pairs={{0,1},{1,0},{2,3},{3,2},{4,5},{5,4},{6,7},{7,6},{8,9},{9,8},{10,11... | collective-permute-start | bytes 786440 | tf_op jit(solution)/shard_map/ppermute | solution.py:384
  78.3 85.7 %all-to-all-start = ((bf16[128,16,256]{0,2,1:T(8,128)(2,1)}), bf16[128,16,256]{0,2,1:T(8,128)(2,1)}, u32[]{:S(2)}, u32[]{:S(2)}) async-start(bf16[128,16,256]{0,2,1:T(8,128)(2,1)} %bitcast.14), calls=%async_computation | async-start | bytes 2097152 | tf_op jit(solution)/shard_map/all_to_all | solution.py:477
  83.4 92.0 %all-gather.3.cloned.1.call-start = ((), (), s32[]{:S(2)}) async-start(), calls=%async_computation.1 | async-start | bytes 2228224 | tf_op jit(solution)/shard_map/all_gather | solution.py:403
  85.4 5.3 %copy-start.8 = (bf16[512,256]{0,1:T(8,128)(2,1)S(1)}, bf16[512,256]{0,1:T(8,128)(2,1)}, u32[]{:S(2)}) copy-start(bf16[512,256]{0,1:T(8,128)(2,1)} %copy-done.7) | copy-start | bytes 786436
  91.7 2.9 %copy-start.4 = (bf16[512,128]{0,1:T(8,128)(2,1)S(1)}, bf16[512,128]{0,1:T(8,128)(2,1)}, u32[]{:S(2)}) copy-start(bf16[512,128]{0,1:T(8,128)(2,1)} %get-tuple-element.58) | copy-start | bytes 393220
  93.4 9.4 %copy-start.2 = (bf16[512,4096]{1,0:T(8,128)(2,1)S(1)}, bf16[512,4096]{1,0:T(8,128)(2,1)}, u32[]{:S(2)}) copy-start(bf16[512,4096]{1,0:T(8,128)(2,1)} %copy-done.1) | copy-start | bytes 12582916
  93.5 9.2 %collective-permute-start.3 = (bf16[512,256]{0,1:T(8,128)(2,1)S(1)}, bf16[512,256]{0,1:T(8,128)(2,1)S(1)}, u32[]{:S(2)}, u32[]{:S(2)}) collective-permute-start(bf16[512,256]{0,1:T(8,128)(2,1)S(1)} %pad_maximum_fusion.2), channel_id=1, source_target_pairs={{0,1},{1,0},{2,3},{3,2},{4,5},{5,4},{6,7},{7,6},{8,9},{9,8},{10,11... | collective-permute-start | bytes 786440 | tf_op jit(solution)/shard_map/ppermute | solution.py:384
  97.6 69.3 %collective-permute-start.5 = (bf16[128,2048]{1,0:T(8,128)(2,1)}, bf16[128,2048]{1,0:T(8,128)(2,1)}, u32[]{:S(2)}, u32[]{:S(2)}) collective-permute-start(bf16[128,2048]{1,0:T(8,128)(2,1)} %convolution_convert_fusion.1), channel_id=1, source_target_pairs={{0,1},{1,0},{2,3},{3,2},{4,5},{5,4},{6,7},{7,6},{8,9},{9,8},{10,11... | collective-permute-start | bytes 1572872 | tf_op jit(solution)/shard_map/ppermute | solution.py:384
  98.9 12.7 %copy-start.6 = (bf16[1,512,128]{1,2,0:T(8,128)(2,1)}, bf16[1,512,128]{1,2,0:T(8,128)(2,1)S(1)}, u32[]{:S(2)}) copy-start(bf16[1,512,128]{1,2,0:T(8,128)(2,1)S(1)} %fusion.37) | copy-start | bytes 393220
  107.7 62.3 %collective-permute-start.4 = (bf16[3,2048,128]{1,2,0:T(8,128)(2,1)}, bf16[3,2048,128]{1,2,0:T(8,128)(2,1)}, u32[]{:S(2)}, u32[]{:S(2)}) collective-permute-start(bf16[3,2048,128]{1,2,0:T(8,128)(2,1)} %fusion.5), channel_id=1, source_target_pairs={{0,1},{1,0},{2,3},{3,2},{4,5},{5,4},{6,7},{7,6},{8,9},{9,8},{10,11... | collective-permute-start | bytes 4718600 | tf_op jit(solution)/shard_map/ppermute | solution.py:384
  113.5 46.2 %copy-start.10 = (bf16[512,256]{1,0:T(8,128)(2,1)S(1)}, bf16[512,256]{1,0:T(8,128)(2,1)}, u32[]{:S(2)}) copy-start(bf16[512,256]{1,0:T(8,128)(2,1)} %refs_0_.1) | copy-start | bytes 786436
  113.5 46.2 %copy-start.12 = (f32[1,256]{1,0:T(1,128)S(1)}, f32[1,256]{1,0:T(1,128)}, u32[]{:S(2)}) copy-start(f32[1,256]{1,0:T(1,128)} %get-tuple-element.49) | copy-start | bytes 3076
  113.5 46.2 %copy-start.13 = (f32[1,256]{1,0:T(1,128)S(1)}, f32[1,256]{1,0:T(1,128)}, u32[]{:S(2)}) copy-start(f32[1,256]{1,0:T(1,128)} %get-tuple-element.50) | copy-start | bytes 3076
  113.5 46.2 %copy-start.14 = (pred[512]{0:T(512)(128)(4,1)S(1)}, pred[512]{0:T(512)(128)(4,1)}, u32[]{:S(2)}) copy-start(pred[512]{0:T(512)(128)(4,1)} %get-tuple-element.47) | copy-start | bytes 1540
  161.8 4.5 %collective-permute-start.6 = (f32[2,256]{1,0:T(2,128)S(1)}, f32[2,256]{1,0:T(2,128)S(1)}, u32[]{:S(2)}, u32[]{:S(2)}) collective-permute-start(f32[2,256]{1,0:T(2,128)S(1)} %pad_maximum_fusion.3), channel_id=1, source_target_pairs={{0,1},{1,0},{2,3},{3,2},{4,5},{5,4},{6,7},{7,6},{8,9},{9,8},{10,11... | collective-permute-start | bytes 6152 | tf_op jit(solution)/shard_map/ppermute | solution.py:384
  (4 other events, 6.5 us)
Sparse Core Ops, SparseCore 0:
  10.1 59.6 all-gather.4
  92.8 45.4 all-gather.2

commit v3 on v2

--- a/solution.py
+++ b/solution.py
@@ -399,10 +399,6 @@
     return total
 
 
-def gather_features(block):
-    return lax.all_gather(block, ("gx", "gy"), axis=1, tiled=True)
-
-
 def per_device(layer_input, modality, image_spans, norm_gain, w_qkv, w_out, grad_out):
     f32, bf16 = jnp.float32, jnp.bfloat16
     tok_rows, local_width = layer_input.shape
@@ -415,8 +411,7 @@
 
     w_blocks = ring_blocks(w_qkv)
     wo_blocks = ring_blocks(w_out)
-    x_full, gain_full = gather_kernel([layer_input, norm_gain], 1)
-    go_full = gather_features(grad_out)
+    x_full, gain_full, go_full = gather_kernel([layer_input, norm_gain, grad_out], 1)
     full_width = x_full.shape[1]
 
     x_f = x_full.astype(f32)
@@ -470,7 +465,7 @@
         for step in range(count)
     ).astype(bf16)
 
-    all_heads = gather_features(attended)
+    (all_heads,) = gather_kernel([attended], 3)
     wo_rows = jnp.zeros((head_dim, full_width), bf16)
     for step in range(count):
         wo_rows = lax.dynamic_update_slice_in_dim(wo_rows, wo_blocks[step], owners[step] * half, 1)

time: 186 us -> 196 us (1.054)
  Pallas kernels: 95.2 us -> 113 us
  between operations: 14.5 us -> 1.04 us
  waiting for transfers between devices: 4.23 us -> 11.9 us
    pallas_call x1 -> x2, Pallas kernels: 49.8 us -> 75.4 us  [gather_kernel(): pl.pallas_call(functools.partial(gather_body, arity, nx, nz), out_shape=[...]
    ppermute x7, waiting for transfers between devices: 3.5 us -> 11.9 us  [shift_ring(): lax.ppermute(block, 'gz', [(src, (src + step) % count) for src in range(c...]
    pallas_call x1, Pallas kernels: 45.5 us -> 38 us  [reduce_kernel(): pl.pallas_call(functools.partial(reduce_body, nx, nz), out_shape=[jax.Sha...]
    dot_general x2, matrix products: 3.99 us -> 6.64 us  [per_device(): jnp.einsum('mth,mch->tc', grads, w_blocks[step], preferred_element_type=f32)]
    dot_general x2, matrix products: 6.04 us -> 3.5 us  [per_device(): lax.dot_general(attended, columns_of(go_full, step), (((0,), (0,)), ((),...]
    unnamed x39 -> x29, local copies, waits for them, and re-layouts: 7.46 us -> 5.46 us
    broadcast_in_dim x1, local copies, waits for them, and re-layouts: 0.5 us -> 2.46 us  [per_device(): partial = jnp.zeros((tok_rows, full_width), bf16)]
  transfers between devices with their start and end apart: 10 -> 8, of which waited for: 1 -> 2; matrix products, arithmetic and copies ran while one was open for 28% -> 25% of each run, Pallas kernels for 51% -> 58%
where the time goes in v3:
time: 196 us; the launch traced here: 195 us
  Pallas kernels  113 us (58%)
  matrix products  30.8 us (16%)
  starting transfers between devices  14 us (7%)
  local copies, waits for them, and re-layouts  12.6 us (6%)
  waiting for transfers between devices  11.9 us (6%)
  other arithmetic  11.8 us (6%)
    pallas_call x2, Pallas kernels, gather_kernel(): pl.pallas_call(functools.partial(gather_body, arity, nx, nz), out_shape=[...  75.4 us
    pallas_call x1, Pallas kernels, reduce_kernel(): pl.pallas_call(functools.partial(reduce_body, nx, nz), out_shape=[jax.Sha...  38 us
    ppermute x7, waiting for transfers between devices, shift_ring(): lax.ppermute(block, 'gz', [(src, (src + step) % count) for src in range(c...  11.9 us
    ppermute x7, starting transfers between devices, shift_ring(): lax.ppermute(block, 'gz', [(src, (src + step) % count) for src in range(c...  9.04 us
    dot_general x2, matrix products, per_device(): jnp.einsum('mth,mch->tc', grads, w_blocks[step], preferred_element_type=f32)  6.64 us
    unnamed x29, local copies, waits for them, and re-layouts  5.46 us
    dot_general x2, matrix products, per_device(): jnp.einsum('tc,mth->mch', columns_of(normed, step), grads, preferred_elem...  5.16 us
    unnamed x2, matrix products  5.1 us
  transfers between devices with their start and end apart: 8, of which 2 were waited for; matrix products, arithmetic and copies ran while one was open for 25% of the time, Pallas kernels for 58%

profile of v3, /device:TPU:0, one launch (start us, length us, event | category | flops | bytes accessed | tf_op | source)
XLA Modules:
  0.0 195.5 jit_solution(13747604573671689913)
XLA Ops:
  2.0 3.1 %collective-permute-start.2 = (bf16[128,2048]{0,1:T(8,128)(2,1)S(1)}, bf16[128,2048]{0,1:T(8,128)(2,1)S(1)}, u32[]{:S(2)}, u32[]{:S(2)}) collective-permute-start(bf16[128,2048]{0,1:T(8,128)(2,1)S(1)} %copy.55), channel_id=1, source_target_pairs={{0,1},{1,0},{2,3},{3,2},{4,5},{5,4},{6,7},{7,6},{8,9},{9,8},{10,11... | collective-permute-start | bytes 1572872 | tf_op jit(solution)/shard_map/ppermute | solution.py:384
  5.0 1.7 copy.51
  6.9 55.0 %gather_features.2 = (bf16[512,4096]{1,0:T(8,128)(2,1)}, f32[2,4096]{1,0:T(2,128)}, bf16[512,4096]{1,0:T(8,128)(2,1)}) custom-call(bf16[512,256]{1,0:T(8,128)(2,1)} %refs_0_.1, f32[2,256]{1,0:T(2,128)} %refs_1_.1, bf16[512,256]{1,0:T(8,128)(2,1)} %refs_2_.1), custom_call_target="tpu_custom_call" | custom-call | flops 42106880000 | bytes 8388608 | tf_op jit(solution)/shard_map/gather_features/pallas_call | solution.py:181
  62.8 3.1 %fusion = f32[512]{0:T(512)S(1)} fusion(bf16[512,4096]{1,0:T(8,128)(2,1)} %get-tuple-element.10), kind=kLoop, calls=%fused_computation.2 | loop fusion | flops 6290944 | bytes 4196352 | tf_op jit(solution)/shard_map/reduce_sum | solution.py:418
  66.6 2.3 %fusion.13 = f32[512,128]{1,0:T(8,128)S(1)} fusion(bf16[128,2048]{1,0:T(8,128)(2,1)S(1)} %copy-done.3, bf16[512,4096]{1,0:T(8,128)(2,1)} %get-tuple-element.12, s32[]{:T(128)S(6)} %select_n.51), kind=kOutput, calls=%fused_computation.20 | convolution fusion | flops 268435456 | bytes 2883588 | tf_op jit(solution)/shard_map/dot_general | solution.py:438
  68.9 3.3 %fusion.2 = bf16[512,4096]{1,0:T(8,128)(2,1)S(1)} fusion(bf16[512,4096]{1,0:T(8,128)(2,1)} %get-tuple-element.10, f32[4096]{0:T(1024)S(1)} %bitcast.94, f32[4096]{0:T(1024)S(1)} %bitcast.93, f32[512]{0:T(512)S(1)} %add_rsqrt_fusion, pred[512]{0:T(512)(128)(4,1)S(1)} %get-tuple-element.50), kind=kLoop, calls=%fused_computation.4 | loop fusion | flops 10485760 | bytes 8423936 | tf_op jit(solution)/shard_map/convert_element_type | solution.py:422
  74.7 1.9 fusion.19
  77.4 5.0 %all-to-all-start = ((bf16[128,16,256]{0,2,1:T(8,128)(2,1)}), bf16[128,16,256]{0,2,1:T(8,128)(2,1)S(1)}, u32[]{:S(2)}, u32[]{:S(2)}) async-start(bf16[128,16,256]{0,2,1:T(8,128)(2,1)} %bitcast.14), calls=%async_computation | async-start | bytes 2097152 | tf_op jit(solution)/shard_map/all_to_all | solution.py:472
  82.4 3.2 %fusion.16 = f32[512,384]{0,1:S(1)} fusion(bf16[2048,384]{0,1:T(8,128)(2,1)} %bitcast.8, bf16[512,4096]{1,0:T(8,128)(2,1)} %copy-done.1, s32[]{:T(128)S(6)} %select_n.52), kind=kOutput, calls=%fused_computation.23 | convolution fusion | flops 805306368 | bytes 4456452
  85.9 1.6 collective-permute-start.1
  88.7 5.8 %collective-permute-done.1 = bf16[512,256]{0,1:T(8,128)(2,1)S(1)} collective-permute-done((bf16[512,256]{0,1:T(8,128)(2,1)S(1)}, bf16[512,256]{0,1:T(8,128)(2,1)S(1)}, u32[]{:S(2)}, u32[]{:S(2)}) %collective-permute-start.1) | collective-permute-done | bytes 262176 | tf_op jit(solution)/shard_map/ppermute | solution.py:384
  98.2 1.6 collective-permute-start.3
  101.4 6.1 %collective-permute-done.3 = bf16[512,256]{0,1:T(8,128)(2,1)S(1)} collective-permute-done((bf16[512,256]{0,1:T(8,128)(2,1)S(1)}, bf16[512,256]{0,1:T(8,128)(2,1)S(1)}, u32[]{:S(2)}, u32[]{:S(2)}) %collective-permute-start.3) | collective-permute-done | bytes 262176 | tf_op jit(solution)/shard_map/ppermute | solution.py:384
  108.3 2.1 %fusion.5 = bf16[3,2048,128]{1,2,0:T(8,128)(2,1)} fusion(bf16[512,4096]{1,0:T(8,128)(2,1)S(1)} %copy-done.2, s32[]{:T(128)S(6)} %select_n.52, bf16[1,512,128]{1,2,0:T(8,128)(2,1)S(1)} %get-tuple-element.46, bf16[1,512,128]{1,2,0:T(8,128)(2,1)S(1)} %get-tuple-element.45, bf16[1,512,128]{1,2,0:T(8,128)(2,1)S(1)} %fusion.37), kind=kOutput, calls=%fused_computation.11 | convolution fusion | flops 806486016 | bytes 4063236 | tf_op jit(solution)/shard_map/tc,mth->mch/dot_general | solution.py:521
  110.4 2.5 %broadcast_in_dim.148 = bf16[512,4096]{1,0:T(8,128)(2,1)} broadcast(bf16[]{:T(256)} %constant.43.clone.1), dimensions={} | broadcast | bytes 4194306 | tf_op jit(solution)/shard_map/broadcast_in_dim | solution.py:509
  112.9 2.7 %fusion.3 = bf16[512,4096]{1,0:T(8,128)(2,1)} fusion(bf16[512,4096]{1,0:T(8,128)(2,1)} %broadcast_in_dim.148, s32[]{:T(128)S(6)} %select_n.51, bf16[3,2048,128]{2,1,0:T(8,128)(2,1)S(1)} %copy-done.4, bf16[1,512,128]{1,2,0:T(8,128)(2,1)S(1)} %get-tuple-element.46, bf16[1,512,128]{1,2,0:T(8,128)(2,1)S(1)} %get-tuple-element.45, ...), kind=kOutput, calls=%fused_computation.8 | convolution fusion | flops 806748160 | bytes 4063236 | tf_op jit(solution)/shard_map/mth,mch->tc/dot_general | solution.py:513
  117.0 4.0 %fusion.4.part = bf16[512,4096]{1,0:T(8,128)(2,1)} fusion(bf16[512,4096]{1,0:T(8,128)(2,1)} %fusion.3, s32[]{:T(128)S(6)} %select_n.52, bf16[3,2048,128]{1,2,0:T(8,128)(2,1)} %collective-permute-done, bf16[1,512,128]{1,2,0:T(8,128)(2,1)S(1)} %get-tuple-element.46, bf16[1,512,128]{1,2,0:T(8,128)(2,1)S(1)} %get-tuple-element.45, ...), kind=kOutput, calls=%fused_computation.9 | convolution fusion | flops 806748160 | bytes 4063236 | tf_op jit(solution)/shard_map/mth,mch->tc/dot_general | solution.py:513
  121.0 38.0 %reduce_features.1 = (f32[512,256]{1,0:T(8,128)}, f32[4,128]{1,0:T(4,128)}) custom-call(bf16[512,4096]{1,0:T(8,128)(2,1)} %fusion.4.part, f32[4,128]{1,0:T(4,128)} %bitcast.101), custom_call_target="tpu_custom_call" | custom-call | flops 25165824000 | bytes 8388608 | tf_op jit(solution)/shard_map/reduce_features/pallas_call | solution.py:351
  159.7 2.1 %select_reduce_fusion.1 = (f32[256]{0:T(256)S(1)}, f32[256]{0:T(256)S(1)}, bf16[512,256]{1,0:T(8,128)(2,1)}) fusion(f32[512,256]{1,0:T(8,128)} %get-tuple-element.13, bf16[512,256]{1,0:T(8,128)(2,1)S(1)} %copy-done.8, f32[512]{0:T(512)S(1)} %add_rsqrt_fusion, pred[512]{0:T(512)(128)(4,1)S(1)} %copy-done.9, pred[512]{0:T(512)(128)(4,1)S(1)} %get-tuple-element.50, ...), kind=kLoop, calls=%fused_computation.62 | loop fusion | flops 1703424 | bytes 1057792 | tf_op jit(solution)/shard_map/reduce_sum | solution.py:535
  162.5 20.4 %gather_features.3 = bf16[512,2048]{1,0:T(8,128)(2,1)} custom-call(bf16[512,128]{1,0:T(8,128)(2,1)} %copy-done.5), custom_call_target="tpu_custom_call" | custom-call | flops 10485760000 | bytes 8388608 | tf_op jit(solution)/shard_map/gather_features/pallas_call | solution.py:181
  183.5 3.0 %convert_add_fusion = f32[128,2048]{1,0:T(8,128)} fusion(bf16[128,2048]{1,0:T(8,128)(2,1)S(1)} %collective-permute-done.5, bf16[512,128]{1,0:T(8,128)(2,1)S(1)} %copy-done.6, bf16[512,4096]{1,0:T(8,128)(2,1)} %get-tuple-element.12, s32[]{:T(128)S(6)} %select_n.51), kind=kOutput, calls=%fused_computation.52 | convolution fusion | flops 268959744 | bytes 3801092 | tf_op jit(solution)/shard_map/dot_general | solution.py:476
  187.1 3.0 %convolution_convert_fusion.2 = bf16[512,256]{1,0:T(8,128)(2,1)} fusion(bf16[512,2048]{1,0:T(8,128)(2,1)} %gather_features.3, bf16[2048,256]{1,0:T(8,128)(2,1)S(1)} %bitcast.90), kind=kOutput, calls=%fused_computation.40 | convolution fusion | flops 537001984 | bytes 3407872 | tf_op jit(solution)/shard_map/dot_general | solution.py:473
  190.1 3.0 %bitcast_add_fusion = f32[3,2048,128]{1,2,0:T(8,128)S(1)} fusion(bf16[3,2048,128]{1,2,0:T(8,128)(2,1)} %collective-permute-done.4, bf16[512,4096]{1,0:T(8,128)(2,1)} %copy-done.1, s32[]{:T(128)S(6)} %select_n.51, bf16[1,512,128]{1,2,0:T(8,128)(2,1)S(1)} %get-tuple-element.46, bf16[1,512,128]{1,2,0:T(8,128)(2,1)S(1)} %get-tuple-element.45, ...), kind=kOutput, calls=%fused_computation.7 | convolution fusion | flops 807272448 | bytes 7208964 | tf_op jit(solution)/shard_map/tc,mth->mch/dot_general | solution.py:521
  193.1 2.4 %copy.65 = f32[3,2048,128]{2,1,0:T(8,128)} copy(f32[3,2048,128]{1,2,0:T(8,128)S(1)} %bitcast_add_fusion) | data formatting | bytes 6291456
  (81 shorter events, 17.7 us)
Async XLA Ops:
  0.6 6.2 %copy-start.11 = (f32[2,256]{1,0:T(2,128)S(1)}, f32[2,256]{1,0:T(2,128)}, u32[]{:S(2)}) copy-start(f32[2,256]{1,0:T(2,128)} %refs_1_.1) | copy-start | bytes 6148
  2.0 74.6 %collective-permute-start.2 = (bf16[128,2048]{0,1:T(8,128)(2,1)S(1)}, bf16[128,2048]{0,1:T(8,128)(2,1)S(1)}, u32[]{:S(2)}, u32[]{:S(2)}) collective-permute-start(bf16[128,2048]{0,1:T(8,128)(2,1)S(1)} %copy.55), channel_id=1, source_target_pairs={{0,1},{1,0},{2,3},{3,2},{4,5},{5,4},{6,7},{7,6},{8,9},{9,8},{10,11... | collective-permute-start | bytes 1572872 | tf_op jit(solution)/shard_map/ppermute | solution.py:384
  6.8 75.6 %collective-permute-start = (bf16[3,2048,128]{1,2,0:T(8,128)(2,1)S(1)}, bf16[3,2048,128]{1,2,0:T(8,128)(2,1)}, u32[]{:S(2)}, u32[]{:S(2)}) collective-permute-start(bf16[3,2048,128]{1,2,0:T(8,128)(2,1)S(1)} %copy.51), channel_id=1, source_target_pairs={{0,1},{1,0},{2,3},{3,2},{4,5},{5,4},{6,7},{7,6},{8,9},{9,8},{10,11... | collective-permute-start | bytes 4718600 | tf_op jit(solution)/shard_map/ppermute | solution.py:384
  61.9 4.0 %copy-start.10 = (s32[512]{0:T(512)S(1)}, s32[512]{0:T(512)}, u32[]{:S(2)}) copy-start(s32[512]{0:T(512)} %param.8) | copy-start | bytes 6148
  61.9 4.5 %copy-start.12 = (s32[2,8]{1,0:T(2,128)S(1)}, s32[2,8]{1,0:T(2,128)}, u32[]{:S(2)}) copy-start(s32[2,8]{1,0:T(2,128)} %param.9) | copy-start | bytes 196
  61.9 4.7 %copy-start.3 = (bf16[128,2048]{1,0:T(8,128)(2,1)S(1)}, bf16[128,2048]{1,0:T(8,128)(2,1)}, u32[]{:S(2)}) copy-start(bf16[128,2048]{1,0:T(8,128)(2,1)} %param.12) | copy-start | bytes 1572868
  72.2 4.3 %copy-start.1 = (bf16[512,4096]{1,0:T(8,128)(2,1)}, bf16[512,4096]{1,0:T(8,128)(2,1)S(1)}, u32[]{:S(2)}) copy-start(bf16[512,4096]{1,0:T(8,128)(2,1)S(1)} %fusion.2) | copy-start | bytes 12582916
  77.4 109.2 %all-to-all-start = ((bf16[128,16,256]{0,2,1:T(8,128)(2,1)}), bf16[128,16,256]{0,2,1:T(8,128)(2,1)S(1)}, u32[]{:S(2)}, u32[]{:S(2)}) async-start(bf16[128,16,256]{0,2,1:T(8,128)(2,1)} %bitcast.14), calls=%async_computation | async-start | bytes 2097152 | tf_op jit(solution)/shard_map/all_to_all | solution.py:472
  82.4 3.2 %copy-start.7 = (f32[512,384]{0,1:S(1)}, f32[512,384]{0,1}, u32[]{:S(2)}) copy-start(f32[512,384]{0,1} %fusion.19) | copy-start | bytes 2359300
  82.4 5.1 %copy-start = (bf16[512,4096]{1,0:T(8,128)(2,1)S(1)}, bf16[512,4096]{1,0:T(8,128)(2,1)}, u32[]{:S(2)}) copy-start(bf16[512,4096]{1,0:T(8,128)(2,1)} %get-tuple-element.12) | copy-start | bytes 12582916
  85.9 8.7 %collective-permute-start.1 = (bf16[512,256]{0,1:T(8,128)(2,1)S(1)}, bf16[512,256]{0,1:T(8,128)(2,1)S(1)}, u32[]{:S(2)}, u32[]{:S(2)}) collective-permute-start(bf16[512,256]{0,1:T(8,128)(2,1)S(1)} %pad_maximum_fusion.1), channel_id=1, source_target_pairs={{0,1},{1,0},{2,3},{3,2},{4,5},{5,4},{6,7},{7,6},{8,9},{9,8},{10,11... | collective-permute-start | bytes 786440 | tf_op jit(solution)/shard_map/ppermute | solution.py:384
  96.5 3.3 %copy-start.5 = (bf16[512,128]{1,0:T(8,128)(2,1)}, bf16[512,128]{1,0:T(8,128)(2,1)S(1)}, u32[]{:S(2)}) copy-start(bf16[512,128]{1,0:T(8,128)(2,1)S(1)} %get-tuple-element.60.refs_0_) | copy-start | bytes 393220
  98.2 9.2 %collective-permute-start.3 = (bf16[512,256]{0,1:T(8,128)(2,1)S(1)}, bf16[512,256]{0,1:T(8,128)(2,1)S(1)}, u32[]{:S(2)}, u32[]{:S(2)}) collective-permute-start(bf16[512,256]{0,1:T(8,128)(2,1)S(1)} %pad_maximum_fusion.2), channel_id=1, source_target_pairs={{0,1},{1,0},{2,3},{3,2},{4,5},{5,4},{6,7},{7,6},{8,9},{9,8},{10,11... | collective-permute-start | bytes 786440 | tf_op jit(solution)/shard_map/ppermute | solution.py:384
  99.8 8.5 %copy-start.2 = (bf16[512,4096]{1,0:T(8,128)(2,1)S(1)}, bf16[512,4096]{1,0:T(8,128)(2,1)}, u32[]{:S(2)}) copy-start(bf16[512,4096]{1,0:T(8,128)(2,1)} %copy-done.1) | copy-start | bytes 12582916
  100.2 83.3 %collective-permute-start.5 = (bf16[128,2048]{1,0:T(8,128)(2,1)S(1)}, bf16[128,2048]{1,0:T(8,128)(2,1)S(1)}, u32[]{:S(2)}, u32[]{:S(2)}) collective-permute-start(bf16[128,2048]{1,0:T(8,128)(2,1)S(1)} %convolution_convert_fusion.1), channel_id=1, source_target_pairs={{0,1},{1,0},{2,3},{3,2},{4,5},{5,4},{6,7},{7,6},{8,9},{9,8},{10,11... | collective-permute-start | bytes 1572872 | tf_op jit(solution)/shard_map/ppermute | solution.py:384
  110.4 2.5 %copy-start.4 = (bf16[3,2048,128]{2,1,0:T(8,128)(2,1)S(1)}, bf16[3,2048,128]{2,1,0:T(8,128)(2,1)}, u32[]{:S(2)}) copy-start(bf16[3,2048,128]{2,1,0:T(8,128)(2,1)} %param.11) | copy-start | bytes 4718596
  115.5 74.6 %collective-permute-start.4 = (bf16[3,2048,128]{1,2,0:T(8,128)(2,1)}, bf16[3,2048,128]{1,2,0:T(8,128)(2,1)}, u32[]{:S(2)}, u32[]{:S(2)}) collective-permute-start(bf16[3,2048,128]{1,2,0:T(8,128)(2,1)} %fusion.5), channel_id=1, source_target_pairs={{0,1},{1,0},{2,3},{3,2},{4,5},{5,4},{6,7},{7,6},{8,9},{9,8},{10,11... | collective-permute-start | bytes 4718600 | tf_op jit(solution)/shard_map/ppermute | solution.py:384
  121.0 38.7 %copy-start.8 = (bf16[512,256]{1,0:T(8,128)(2,1)S(1)}, bf16[512,256]{1,0:T(8,128)(2,1)}, u32[]{:S(2)}) copy-start(bf16[512,256]{1,0:T(8,128)(2,1)} %refs_0_.1) | copy-start | bytes 786436
  121.0 38.7 %copy-start.9 = (pred[512]{0:T(512)(128)(4,1)S(1)}, pred[512]{0:T(512)(128)(4,1)}, u32[]{:S(2)}) copy-start(pred[512]{0:T(512)(128)(4,1)} %get-tuple-element.49) | copy-start | bytes 1540
  161.8 21.7 %copy-start.6 = (bf16[512,128]{1,0:T(8,128)(2,1)S(1)}, bf16[512,128]{1,0:T(8,128)(2,1)}, u32[]{:S(2)}) copy-start(bf16[512,128]{1,0:T(8,128)(2,1)} %copy-done.5) | copy-start | bytes 393220
  161.8 21.1 %collective-permute-start.6 = (f32[2,256]{1,0:T(2,128)S(1)}, f32[2,256]{1,0:T(2,128)S(1)}, u32[]{:S(2)}, u32[]{:S(2)}) collective-permute-start(f32[2,256]{1,0:T(2,128)S(1)} %pad_maximum_fusion.3), channel_id=1, source_target_pairs={{0,1},{1,0},{2,3},{3,2},{4,5},{5,4},{6,7},{7,6},{8,9},{9,8},{10,11... | collective-permute-start | bytes 6152 | tf_op jit(solution)/shard_map/ppermute | solution.py:384
